TPU v7x, 32 devices: a whole 2x2x4 slice. The times are simulated.
32 devices in a mesh: groups: 2 (over y), seq: 4 (over x, core), qset: 4 (over z).
Axes of the slice: x: 2, y: 2, z: 4, core: 2. Of those that a mesh axis runs over, the one named last changes fastest.
Arguments:
- states: bfloat16 [8, 4, 128, 4096], P(('groups', 'qset'), 'seq'), parts along dimension 0, may hold values from -7 to 7
- enc_gain: bfloat16 [4096], replicated, may hold values from 0.25 to 1.75
- dec_states: bfloat16 [16, 64, 4096], P(('groups', 'qset')), parts along dimension 0, may hold values from -7 to 7
- dec_gain: bfloat16 [4096], replicated, may hold values from 0.25 to 1.75
- query_weight: bfloat16 [4096, 4096], P(None, 'seq'), may hold values from -0.375 to 0.375
- key_value_weight: bfloat16 [4096, 2, 4096], P(None, None, 'seq'), may hold values from -0.0625 to 0.0625
- out_weight: bfloat16 [4096, 4096], P('seq'), may hold values from -0.75 to 0.75
- question_of: int32 [8, 4, 1], P('groups'), parts along dimension 0, may hold values from 0 to 7; in each aligned block of 4 rows (0 to 3, 4 to 7, ..., all dimensions but the last counted through in order) at most 2 rows name the same one
Outputs:
- mixed: bfloat16 [16, 64, 4096], P(('groups', 'qset'), None, 'seq'), parts along dimension 0
There are 2 independent parts, one for each index of `groups`. A program takes and returns all parts, laid end to end along the dimension named above; an argument that names none is the same for every part. Nothing has to cross between parts.
Inputs may be any that keep to these rules, and one draw needn't show every extreme that they name: `question_of`: within each index of the first dimension (one source group of 4 passages) at most 2 passages name the same question, and exactly 2 do for some question in some groups; every question is named by at least one passage.
All inputs are finite; a program needn't handle non-finite values.
Results may differ from a plain program's by a relative error of at most 0.014.
The roundings to bfloat16 on the way count: a program that leaves them out, or rounds other values in their place, can miss the bound.
Values may be sent and summed in bfloat16 or wider, within the bound.
No kernel may reach another device: no remote copies, remote signals or barrier semaphores. Data moves between devices by JAX's collectives and lax.ppermute only.
A program may use at most 128 MiB of HBM per device.

v0:
```python
import functools

import jax
import jax.numpy as jnp
from jax import lax
from jax.experimental import pallas as pl
from jax.experimental.pallas import tpu as pltpu
from jax.sharding import PartitionSpec as P


HD = 64
EPSILON = 1e-06
EMPTY = -1e30
LANES = 128
CUTS = (0, 8, 13, 16)


F32 = jnp.float32
BF16 = jnp.bfloat16


def cost(flops, bytes_accessed):
    return pl.CostEstimate(flops=int(flops), bytes_accessed=int(bytes_accessed), transcendentals=0)


def full_spec():
    return pl.BlockSpec(memory_space=pltpu.VMEM)


def enc_norm_kernel(x_ref, g_ref, *out_refs):
    x = x_ref[...].astype(F32)
    scale = lax.rsqrt(jnp.mean(x * x, axis=-1, keepdims=True) + EPSILON)
    gain = g_ref[...].astype(F32)
    block = 0
    for out in out_refs:
        for i in range(out.shape[1] // LANES):
            part = x_ref[:, block * LANES : (block + 1) * LANES].astype(F32)
            out[:, i * LANES : (i + 1) * LANES] = (part * scale * gain[block : block + 1]).astype(BF16)
            block += 1


def enc_norm(x, gain, cuts):
    rows, width = x.shape
    return pl.pallas_call(
        enc_norm_kernel,
        grid=(1,),
        in_specs=[
            pl.BlockSpec((rows, width), lambda i: (0, 0)),
            pl.BlockSpec((width // LANES, LANES), lambda i: (0, 0)),
        ],
        out_specs=[full_spec()] * (len(cuts) - 1),
        out_shape=[jax.ShapeDtypeStruct((rows, b - a), BF16) for a, b in zip(cuts, cuts[1:])],
        cost_estimate=cost(2e10, rows * width * 4),
        compiler_params=pltpu.CompilerParams(vmem_limit_bytes=8 << 20),
        name="enc_norm",
    )(x, gain.reshape(width // LANES, LANES))


def query_kernel(x_hbm, g_ref, w_hbm, out_ref, x_ref, w_ref, rows_ref, sems):
    pieces = sems.shape[0] - 1
    depth = w_ref.shape[0] // pieces
    cuts = [pl.ds(i * depth, depth) for i in range(pieces)]
    copies = [pltpu.make_async_copy(x_hbm, x_ref, sems.at[pieces])] + [
        pltpu.make_async_copy(w_hbm.at[cut], w_ref.at[cut], sems.at[i])
        for i, cut in enumerate(cuts)
    ]
    for copy in copies:
        copy.start()
    copies[0].wait()
    x = x_ref[...].astype(F32)
    scale = lax.rsqrt(jnp.mean(x * x, axis=-1, keepdims=True) + EPSILON)
    gain = g_ref[...].astype(F32)
    for block in range(x_ref.shape[1] // LANES):
        span = slice(block * LANES, (block + 1) * LANES)
        part = x_ref[:, span].astype(F32) * scale * gain[block : block + 1]
        rows_ref[:, span] = part.astype(BF16)
    total = None
    for copy, cut in zip(copies[1:], cuts):
        copy.wait()
        part = jnp.dot(rows_ref[:, cut], w_ref[cut, :], preferred_element_type=F32)
        total = part if total is None else total + part
    out_ref[...] = total.astype(BF16)


def query_rows(x, gain, weight):
    rows, width = x.shape
    cols = weight.shape[1]
    pieces = 8
    return pl.pallas_call(
        query_kernel,
        in_specs=[
            pl.BlockSpec(memory_space=pl.ANY),
            full_spec(),
            pl.BlockSpec(memory_space=pl.ANY),
        ],
        out_specs=full_spec(),
        out_shape=jax.ShapeDtypeStruct((rows, cols), BF16),
        scratch_shapes=[
            pltpu.VMEM((rows, width), BF16),
            pltpu.VMEM((width, cols), BF16),
            pltpu.VMEM((rows, width), BF16),
            pltpu.SemaphoreType.DMA((pieces + 1,)),
        ],
        cost_estimate=cost(3e9, width * cols * 2),
        compiler_params=pltpu.CompilerParams(vmem_limit_bytes=14 << 20),
        name="query_rows",
    )(x, gain.reshape(width // LANES, LANES), weight)


def sum_kernel(index, res_ref, *refs):
    out_ref = refs[-1]
    per = out_ref.shape[0]
    count = len(refs[:-1]) // per
    for j in range(per):
        total = res_ref[j].astype(F32)
        for ref in refs[j * count : (j + 1) * count]:
            total = total + ref[...].astype(F32)
        out_ref[j] = total.astype(BF16)


def sum_parts(index, residual, parts):
    per, dec_len, _ = residual.shape
    cols = parts[0].shape[1]
    return pl.pallas_call(
        sum_kernel,
        grid_spec=pltpu.PrefetchScalarGridSpec(
            num_scalar_prefetch=1,
            grid=(1,),
            in_specs=[pl.BlockSpec((per, dec_len, cols), lambda i, s: (0, 0, s[0]))]
            + [full_spec()] * len(parts),
            out_specs=pl.BlockSpec((per, dec_len, cols), lambda i, s: (0, 0, 0)),
        ),
        out_shape=jax.ShapeDtypeStruct((per, dec_len, cols), BF16),
        cost_estimate=cost(per * dec_len * cols * 8, per * dec_len * cols * 12),
        compiler_params=pltpu.CompilerParams(vmem_limit_bytes=8 << 20),
        name="sum_parts",
    )(index, residual, *parts)


def load_kernel(cuts, step, src, *refs):
    dests, sems = refs[:-1], refs[-1]
    copies = []
    for a, b, dest in zip(cuts, cuts[1:], dests):
        for low in range(a, b, step):
            size = min(step, b - low)
            copies.append(
                pltpu.make_async_copy(
                    src.at[pl.ds(low, size)], dest.at[pl.ds(low - a, size)], sems.at[len(copies)]
                )
            )
    for copy in copies:
        copy.start()
    for copy in copies:
        copy.wait()


def load(array, cuts, step, limit):
    shapes = [(b - a,) + array.shape[1:] for a, b in zip(cuts, cuts[1:])]
    count = sum(-(-(b - a) // step) for a, b in zip(cuts, cuts[1:]))
    return pl.pallas_call(
        functools.partial(load_kernel, cuts, step),
        in_specs=[pl.BlockSpec(memory_space=pl.ANY)],
        out_specs=[full_spec()] * len(shapes),
        out_shape=[jax.ShapeDtypeStruct(s, BF16) for s in shapes],
        scratch_shapes=[pltpu.SemaphoreType.DMA((count,))],
        cost_estimate=cost(7e9, 2 * array.size),
        compiler_params=pltpu.CompilerParams(vmem_limit_bytes=limit),
    )(array)


def split3(x):
    hi = x.astype(BF16)
    rest = x - hi.astype(F32)
    mid = rest.astype(BF16)
    low = (rest - mid.astype(F32)).astype(BF16)
    return hi, mid, low


def attend_kernel(n_pass, plen, heads, dests, table, *refs):
    q_refs = refs[:dests]
    kv_ref = refs[dests]
    out_refs = refs[dests + 1 : -7]
    qs, score_s, weight_s, part, peak_s, total_s, stat_s = refs[-7:]
    dec_len, cols = out_refs[0].shape[0], heads * HD
    per = len(out_refs) // dests
    wide = score_s.shape[1] // dec_len
    span_w = wide * HD
    groups = cols // span_w
    for i, ref in enumerate(q_refs):
        for j in range(per):
            qs[i * per + j] = ref[j * dec_len : (j + 1) * dec_len, :]
    head_of = lax.broadcasted_iota(jnp.int32, (dec_len, span_w), 1) // HD
    lane = lax.broadcasted_iota(jnp.int32, (dec_len, LANES), 1)
    units = [(p, g) for p in range(n_pass) for g in range(groups)]

    def pick(stacked):
        kept = stacked[:dec_len]
        for h in range(1, wide):
            kept = jnp.where(head_of == h, stacked[h * dec_len : (h + 1) * dec_len], kept)
        return kept

    for p, g in units:
        span = slice(g * span_w, (g + 1) * span_w)
        q = qs[table[0, p], :, span]
        zero = jnp.zeros_like(q)
        stacked = jnp.concatenate([jnp.where(head_of == h, q, zero) for h in range(wide)], axis=0)
        score_s[p * groups + g] = lax.dot_general(
            stacked,
            kv_ref[0, p * plen : (p + 1) * plen, span],
            (((1,), (1,)), ((), ())),
            preferred_element_type=F32,
        )
    for p in range(n_pass):
        peaks = jnp.zeros((dec_len, LANES), F32)
        totals = jnp.zeros((dec_len, LANES), F32)
        for g in range(groups):
            u = p * groups + g
            scores = score_s[u]
            peak = jnp.max(scores, axis=-1, keepdims=True)
            weights = jnp.exp(scores - peak)
            total = jnp.sum(weights, axis=-1, keepdims=True)
            weight_s[u] = weights.astype(BF16)
            span = slice(g * span_w, (g + 1) * span_w)
            peak_s[p, :, span] = pick(jnp.broadcast_to(peak, (peak.shape[0], span_w)))
            total_s[p, :, span] = pick(jnp.broadcast_to(total, (total.shape[0], span_w)))
            for h in range(wide):
                here = lane == g * wide + h
                rows = slice(h * dec_len, (h + 1) * dec_len)
                peaks = jnp.where(here, peak[rows], peaks)
                totals = jnp.where(here, total[rows], totals)
        stat_s[p, 0] = peaks
        stat_s[p, 1] = totals
    for p, g in units:
        span = slice(g * span_w, (g + 1) * span_w)
        summed = jnp.dot(
            weight_s[p * groups + g],
            kv_ref[1, p * plen : (p + 1) * plen, span],
            preferred_element_type=F32,
        )
        part[p, :, span] = pick(summed)

    def put_stats(out, peaks, totals):
        p_hi, p_mid, p_low = split3(peaks)
        t_hi, t_low, _ = split3(totals)
        packed = jnp.concatenate(
            [v[:, :heads] for v in (p_hi, p_mid, p_low, t_hi, t_low)]
            + [jnp.zeros((dec_len, LANES - 5 * heads), BF16)],
            axis=1,
        )
        out[:, cols:] = packed

    for t, out in enumerate(out_refs):
        a, b = table[1, t], table[2, t]

        @pl.when(a < 0)
        def _():
            out[:, :cols] = jnp.zeros((dec_len, cols), BF16)
            put_stats(out, jnp.full((dec_len, LANES), EMPTY, F32), jnp.zeros((dec_len, LANES), F32))

        @pl.when((a >= 0) & (b < 0))
        def _():
            out[:, :cols] = (part[a] / total_s[a]).astype(BF16)
            put_stats(out, stat_s[a, 0], stat_s[a, 1])

        @pl.when((a >= 0) & (b >= 0))
        def _():
            top = jnp.maximum(peak_s[a], peak_s[b])
            f_a, f_b = jnp.exp(peak_s[a] - top), jnp.exp(peak_s[b] - top)
            whole = total_s[a] * f_a + total_s[b] * f_b
            out[:, :cols] = ((part[a] * f_a + part[b] * f_b) / whole).astype(BF16)
            peaks = jnp.maximum(stat_s[a, 0], stat_s[b, 0])
            totals = stat_s[a, 1] * jnp.exp(stat_s[a, 0] - peaks) + stat_s[b, 1] * jnp.exp(
                stat_s[b, 0] - peaks
            )
            put_stats(out, peaks, totals)


def attend(table, queries, kv, n_pass, plen, per, dec_len):
    dests = len(queries)
    cols = queries[0].shape[1]
    heads = cols // HD
    rows = n_pass * dec_len
    wide = min(heads, 4)
    units = n_pass * heads // wide
    return pl.pallas_call(
        functools.partial(attend_kernel, n_pass, plen, heads, dests),
        in_specs=[pl.BlockSpec(memory_space=pltpu.SMEM)] + [full_spec()] * (dests + 1),
        out_specs=[full_spec()] * (dests * per),
        out_shape=[jax.ShapeDtypeStruct((dec_len, cols + LANES), BF16)] * (dests * per),
        scratch_shapes=[
            pltpu.VMEM((dests * per, dec_len, cols), BF16),
            pltpu.VMEM((units, wide * dec_len, plen), F32),
            pltpu.VMEM((units, wide * dec_len, plen), BF16),
            pltpu.VMEM((n_pass, dec_len, cols), F32),
            pltpu.VMEM((n_pass, dec_len, cols), F32),
            pltpu.VMEM((n_pass, dec_len, cols), F32),
            pltpu.VMEM((n_pass, 2, dec_len, LANES), F32),
        ],
        cost_estimate=cost(8 * rows * plen * cols, n_pass * plen * cols * 4),
        compiler_params=pltpu.CompilerParams(vmem_limit_bytes=20 << 20),
        name="attend",
    )(table, *queries, kv)


def project_kernel(heads, parts, order, *refs):
    part_refs = refs[:parts]
    w_ref = refs[parts]
    out_refs = refs[parts + 1 : -1]
    rows_ref = refs[-1]
    dec_len, cols = part_refs[0].shape[0], heads * HD
    row = lax.broadcasted_iota(jnp.int32, (LANES, cols), 0)
    head = lax.broadcasted_iota(jnp.int32, (LANES, cols), 1) // HD
    same = (row % heads == head).astype(F32)
    spread_peak = jnp.where(row < 3 * heads, same, 0.0).astype(BF16)
    spread_total = jnp.where((row >= 3 * heads) & (row < 5 * heads), same, 0.0).astype(BF16)
    stats = jnp.concatenate([ref[:, cols:] for ref in part_refs], axis=0)
    peaks = jnp.dot(stats, spread_peak, preferred_element_type=F32)
    totals = jnp.dot(stats, spread_total, preferred_element_type=F32)
    peaks = [peaks[i * dec_len : (i + 1) * dec_len] for i in range(parts)]
    totals = [totals[i * dec_len : (i + 1) * dec_len] for i in range(parts)]
    top = functools.reduce(jnp.maximum, peaks)
    sizes = [t * jnp.exp(p - top) for p, t in zip(peaks, totals)]
    mixed = functools.reduce(
        jnp.add, [ref[:, :cols].astype(F32) * s for ref, s in zip(part_refs, sizes)]
    )
    rows_ref[...] = (mixed / functools.reduce(jnp.add, sizes)).astype(BF16)
    piece = out_refs[0].shape[1]
    for i, out in enumerate(out_refs):
        cut = pl.ds(pl.multiple_of(order[i] * piece, piece), piece)
        out[...] = jnp.dot(rows_ref[...], w_ref[:, cut], preferred_element_type=F32).astype(BF16)


def project(order, partials, weight):
    parts = len(partials)
    rows, wide = partials[0].shape
    cols = wide - LANES
    heads = cols // HD
    count = order.shape[0]
    piece = weight.shape[1] // count
    return pl.pallas_call(
        functools.partial(project_kernel, heads, parts),
        in_specs=[pl.BlockSpec(memory_space=pltpu.SMEM)] + [full_spec()] * (parts + 1),
        out_specs=[full_spec()] * count,
        out_shape=[jax.ShapeDtypeStruct((rows, piece), BF16)] * count,
        scratch_shapes=[pltpu.VMEM((rows, cols), BF16)],
        cost_estimate=cost(2 * rows * cols * weight.shape[1], cols * weight.shape[1] * 2),
        compiler_params=pltpu.CompilerParams(vmem_limit_bytes=16 << 20),
        name="project",
    )(order, *partials, weight)


def body(
    states, enc_gain, dec_states, dec_gain, query_weight, key_value_weight, out_weight, question_of
):
    width = states.shape[-1]
    plen = states.shape[2]
    n_set = lax.axis_size("qset")
    n_seq = lax.axis_size("seq")
    me_set = lax.axis_index("qset")
    me_seq = lax.axis_index("seq")
    per, dec_len = dec_states.shape[0], dec_states.shape[1]
    chips = n_seq // 2
    chip, core = me_seq // 2, me_seq % 2
    cuts = [width * c // 16 for c in CUTS]

    def seq_move(hop, flip):
        return [(s, 2 * ((s // 2 + hop) % chips) + ((s % 2) ^ flip)) for s in range(n_seq)]

    def set_move(hop):
        return [(s, (s + hop) % n_set) for s in range(n_set)]

    def cross(own):
        return [lax.ppermute(own, "seq", seq_move(hop, 0)) for hop in range(1, chips)]

    def sibling(rows):
        return lax.ppermute(rows, "seq", seq_move(0, 1))

    own = list(enc_norm(states[0, 0], enc_gain, cuts))
    queries = query_rows(dec_states.reshape(per * dec_len, width), dec_gain, query_weight)
    crossed = [cross(rows) for rows in own]
    slot_seq = jnp.stack(
        [2 * ((chip - hop) % chips) + (core ^ f) for hop in range(chips) for f in range(2)]
    )

    all_queries = [queries] + [
        lax.ppermute(queries, "qset", set_move(hop)) for hop in range(1, n_set)
    ]

    passages = lax.dynamic_index_in_dim(question_of[:, :, 0], me_set, 0, keepdims=False)
    passages = passages[slot_seq]
    owner, number = passages // per, passages % per
    query_slot = ((me_set - owner) % n_set) * per + number
    out_slot = ((owner - me_set) % n_set) * per + number
    index = jnp.arange(n_seq, dtype=jnp.int32)
    named = out_slot[None, :] == jnp.arange(n_set * per, dtype=jnp.int32)[:, None]
    high = jnp.max(jnp.where(named, index[None, :], -1), axis=1)
    low = jnp.min(jnp.where(named, index[None, :], n_seq), axis=1)
    first = jnp.where(high >= 0, low, -1)
    second = jnp.where(high > low, high, -1)
    size = max(n_seq, n_set * per)
    table = jnp.stack([jnp.pad(v, (0, size - v.shape[0])) for v in (query_slot, first, second)])

    kv_parts = load(key_value_weight, cuts, 4096, 20 << 20)
    acc, forwarded = None, ()
    for c, weight in enumerate(kv_parts):
        beside = sibling(own[c])
        here, _ = lax.optimization_barrier((crossed[c], (forwarded, acc if c > 1 else ())))
        forwarded = [sibling(rows) for rows in here]
        chunks = [own[c], beside]
        for pair in zip(here, forwarded):
            chunks += pair
        part = jnp.einsum(
            "rd,dkc->rkc", jnp.concatenate(chunks, axis=0), weight, preferred_element_type=F32
        )
        acc = part if acc is None else acc + part
    kv = jnp.transpose(acc.astype(BF16), (1, 0, 2))

    sent = list(attend(table, all_queries, kv, n_seq, plen, per, dec_len))
    out_source, sent[0] = lax.optimization_barrier((out_weight, sent[0]))
    (out_part,) = load(out_source, [0, out_weight.shape[0]], 256, 20 << 20)
    moves = [(hop, f) for hop in range(chips) for f in range(2)]
    order = jnp.stack([2 * ((chip + hop) % chips) + (core ^ f) for hop, f in moves])
    order = order.astype(jnp.int32)

    partials = []
    for j in range(per):
        partials.append(
            [sent[j]]
            + [lax.ppermute(sent[hop * per + j], "qset", set_move(hop)) for hop in range(1, n_set)]
        )
    parts = []
    for j in range(per):
        out = project(order, partials[j], out_part)
        parts += [out[0]] + [
            lax.ppermute(out[i], "seq", seq_move(*moves[i])) for i in range(1, len(moves))
        ]
    return sum_parts(me_seq.reshape(1).astype(jnp.int32), dec_states, parts)


def solution(mesh):
    return jax.shard_map(
        body,
        mesh=mesh,
        in_specs=(
            P(("groups", "qset"), "seq", None, None),
            P(),
            P(("groups", "qset"), None, None),
            P(),
            P(None, "seq"),
            P(None, None, "seq"),
            P("seq", None),
            P("groups", None, None),
        ),
        out_specs=P(("groups", "qset"), None, "seq"),
        check_vma=False,
    )
```

profile of v0, /device:TPU:0, one launch (start us, length us, event | category | flops | bytes accessed | tf_op | source)
XLA Modules:
  0.0 99.6 jit_solution(17175676582299650904)
XLA Ops:
  0.0 1.2 %copy-done.6 = bf16[1,1,128,4096]{3,2,1,0:T(8,128)(2,1)S(1)} copy-done((bf16[1,1,128,4096]{3,2,1,0:T(8,128)(2,1)S(1)}, bf16[1,1,128,4096]{3,2,1,0:T(8,128)(2,1)}, u32[]{:S(2)}) %copy-start.6) | copy-done | bytes 1048600
  2.5 3.0 %collective-permute-start.7 = (bf16[128,1280]{1,0:T(8,128)(2,1)S(1)}, bf16[128,1280]{1,0:T(8,128)(2,1)}, u32[]{:S(2)}, u32[]{:S(2)}) collective-permute-start(bf16[128,1280]{1,0:T(8,128)(2,1)S(1)} %get-tuple-element.33), channel_id=1, source_target_pairs={{0,8},{4,12},{8,0},{12,4},{1,9},{5,13},{9,1},{13,5},{2,10},{6,14},... | collective-permute-start | bytes 983048 | tf_op jit(solution)/shard_map/ppermute | solution.py:373
  6.0 1.7 %collective-permute-start.10 = (bf16[128,768]{1,0:T(8,128)(2,1)S(1)}, bf16[128,768]{1,0:T(8,128)(2,1)S(1)}, u32[]{:S(2)}, u32[]{:S(2)}) collective-permute-start(bf16[128,768]{1,0:T(8,128)(2,1)S(1)} %get-tuple-element.36), channel_id=1, source_target_pairs={{0,8},{4,12},{8,0},{12,4},{1,9},{5,13},{9,1},{13,5},{2,10},{6,14},... | collective-permute-start | bytes 589832 | tf_op jit(solution)/shard_map/ppermute | solution.py:373
  8.7 5.8 %copy-done.3 = bf16[4096,2,1024]{2,1,0:T(2,128)(2,1)S(1)} copy-done((bf16[4096,2,1024]{2,1,0:T(2,128)(2,1)S(1)}, bf16[4096,2,1024]{2,1,0:T(2,128)(2,1)}, u32[]{:S(2)}) %copy-start.3) | copy-done | bytes 16777240
  14.4 1.1 %shard_map.82 = (bf16[2048,2,1024]{2,1,0:T(2,128)(2,1)S(1)}, bf16[1280,2,1024]{2,1,0:T(2,128)(2,1)S(1)}, bf16[768,2,1024]{2,1,0:T(2,128)(2,1)S(1)}) custom-call(bf16[4096,2,1024]{2,1,0:T(2,128)(2,1)S(1)} %copy-done.3), custom_call_target="tpu_custom_call" | custom-call | flops 7000000000 | bytes 16777216 | tf_op jit(solution)/shard_map/pallas_call | solution.py:160
  15.6 9.7 %collective-permute-done.4 = bf16[128,2048]{1,0:T(8,128)(2,1)S(1)} collective-permute-done((bf16[128,2048]{1,0:T(8,128)(2,1)S(1)}, bf16[128,2048]{1,0:T(8,128)(2,1)S(1)}, u32[]{:S(2)}, u32[]{:S(2)}) %collective-permute-start.4) | collective-permute-done | bytes 524320 | tf_op jit(solution)/shard_map/ppermute | solution.py:373
  25.4 3.4 %copy-done.4 = bf16[4096,1024]{1,0:T(8,128)(2,1)S(1)} copy-done((bf16[4096,1024]{1,0:T(8,128)(2,1)S(1)}, bf16[4096,1024]{1,0:T(8,128)(2,1)}, u32[]{:S(2)}) %copy-start.4) | copy-done | bytes 8388632
  28.7 3.0 %query_rows.1.refs_0_ = bf16[128,1024]{1,0:T(8,128)(2,1)S(1)} custom-call(bf16[128,4096]{1,0:T(8,128)(2,1)S(1)} %bitcast.36, bf16[32,128]{1,0:T(8,128)(2,1)S(1)} %bitcast.39, bf16[4096,1024]{1,0:T(8,128)(2,1)S(1)} %copy-done.4), custom_call_target="tpu_custom_call" | custom-call | flops 3000000000 | bytes 8388608 | tf_op jit(solution)/shard_map/query_rows/pallas_call | solution.py:89
  32.4 2.1 %collective-permute-start = (bf16[128,1024]{1,0:T(8,128)(2,1)S(1)}, bf16[128,1024]{1,0:T(8,128)(2,1)S(1)}, u32[]{:S(2)}, u32[]{:S(2)}) collective-permute-start(bf16[128,1024]{1,0:T(8,128)(2,1)S(1)} %query_rows.1.refs_0_), channel_id=1, source_target_pairs={{0,1},{1,2},{2,3},{3,0},{4,5},{5,6},{6,7},{7,4},{8,9},{9,10},{10,1... | collective-permute-start | bytes 786440 | tf_op jit(solution)/shard_map/ppermute | solution.py:386
  34.5 4.7 %fusion = f32[512,2,1024]{2,0,1:T(8,128)S(1)} fusion(bf16[2048,2,1024]{2,1,0:T(2,128)(2,1)S(1)} %get-tuple-element.32, bf16[128,2048]{1,0:T(8,128)(2,1)S(1)} %collective-permute-done.5, bf16[128,2048]{1,0:T(8,128)(2,1)S(1)} %collective-permute-done.4, bf16[128,2048]{1,0:T(8,128)(2,1)S(1)} %collective-permute-done.3, bf16[128,2048]{1,0:T(8,128)(2,1)S(1)} %get-tuple-element.31), kind=kOutput, calls=%fused_computation.1 | convolution fusion | flops 4303355904 | bytes 14680064 | tf_op jit(solution)/shard_map/rd,dkc->rkc/dot_general | solution.py:412
  39.1 2.7 %collective-permute-start.1 = (bf16[128,1024]{1,0:T(8,128)(2,1)S(1)}, bf16[128,1024]{1,0:T(8,128)(2,1)S(1)}, u32[]{:S(2)}, u32[]{:S(2)}) collective-permute-start(bf16[128,1024]{1,0:T(8,128)(2,1)S(1)} %query_rows.1.refs_0_), channel_id=1, source_target_pairs={{0,2},{1,3},{2,0},{3,1},{4,6},{5,7},{6,4},{7,5},{8,10},{9,11},{10,... | collective-permute-start | bytes 786440 | tf_op jit(solution)/shard_map/ppermute | solution.py:386
  41.8 1.3 %collective-permute-start.2 = (bf16[128,1024]{1,0:T(8,128)(2,1)S(1)}, bf16[128,1024]{1,0:T(8,128)(2,1)S(1)}, u32[]{:S(2)}, u32[]{:S(2)}) collective-permute-start(bf16[128,1024]{1,0:T(8,128)(2,1)S(1)} %query_rows.1.refs_0_), channel_id=1, source_target_pairs={{0,3},{1,0},{2,1},{3,2},{4,7},{5,4},{6,5},{7,6},{8,11},{9,8},{10,9... | collective-permute-start | bytes 786440 | tf_op jit(solution)/shard_map/ppermute | solution.py:386
  43.1 4.0 %fusion.2 = f32[512,2,1024]{2,0,1:T(8,128)S(1)} fusion(bf16[1280,2,1024]{2,1,0:T(2,128)(2,1)S(1)} %get-tuple-element.35, bf16[128,1280]{1,0:T(8,128)(2,1)S(1)} %collective-permute-done.8, bf16[128,1280]{1,0:T(8,128)(2,1)} %collective-permute-done.7, bf16[128,1280]{1,0:T(8,128)(2,1)} %collective-permute-done.6, bf16[128,1280]{1,0:T(8,128)(2,1)S(1)} %get-tuple-element.33), kind=kOutput, calls=%fused_computation.3 | convolution fusion | flops 2689597440 | bytes 10747904 | tf_op jit(solution)/shard_map/rd,dkc->rkc/dot_general | solution.py:412
  47.2 2.2 %fusion.6.refs_4_ = bf16[2,512,1024]{2,1,0:T(8,128)(2,1)S(1)} fusion(f32[512,2,1024]{2,0,1:T(8,128)S(1)} %fusion, f32[512,2,1024]{2,0,1:T(8,128)S(1)} %fusion.2, bf16[768,2,1024]{2,1,0:T(2,128)(2,1)S(1)} %get-tuple-element.38, bf16[128,768]{1,0:T(8,128)(2,1)S(1)} %collective-permute-done.11, bf16[128,768]{1,0:T(8,128)(2,1)S(1)} %collective-permute-done.10, ...), kind=kOutput, calls=%fused_computation.8 | convolution fusion | flops 1616904192 | bytes 14417920 | tf_op jit(solution)/shard_map/rd,dkc->rkc/dot_general | solution.py:412
  49.4 5.5 %collective-permute-done.1.refs_2_ = bf16[128,1024]{1,0:T(8,128)(2,1)S(1)} collective-permute-done((bf16[128,1024]{1,0:T(8,128)(2,1)S(1)}, bf16[128,1024]{1,0:T(8,128)(2,1)S(1)}, u32[]{:S(2)}, u32[]{:S(2)}) %collective-permute-start.1) | collective-permute-done | bytes 262176 | tf_op jit(solution)/shard_map/ppermute | solution.py:386
  54.9 3.0 %attend.1 = (bf16[64,1152]{1,0:T(8,128)(2,1)S(1)}, bf16[64,1152]{1,0:T(8,128)(2,1)S(1)}, bf16[64,1152]{1,0:T(8,128)(2,1)S(1)}, bf16[64,1152]{1,0:T(8,128)(2,1)S(...) custom-call(s32[3,8]{1,0:T(4,128)S(1)} %pad_add_fusion.table, ...), custom_call_target="tpu_custom_call" | custom-call | flops 268435456 | bytes 2097152 | tf_op jit(solution)/shard_map/attend/pallas_call | solution.py:285
  57.9 5.8 %collective-permute-start.18 = (bf16[64,1152]{1,0:T(8,128)(2,1)S(1)}, bf16[64,1152]{1,0:T(8,128)(2,1)S(1)}, u32[]{:S(2)}, u32[]{:S(2)}) collective-permute-start(bf16[64,1152]{1,0:T(8,128)(2,1)S(1)} %get-tuple-element.50), channel_id=1, source_target_pairs={{0,1},{1,2},{2,3},{3,0},{4,5},{5,6},{6,7},{7,4},{8,9},{9,10},{10,1... | collective-permute-start | bytes 442376 | tf_op jit(solution)/shard_map/ppermute | solution.py:429
  63.7 2.1 %collective-permute-start.19 = (bf16[64,1152]{1,0:T(8,128)(2,1)S(1)}, bf16[64,1152]{1,0:T(8,128)(2,1)S(1)}, u32[]{:S(2)}, u32[]{:S(2)}) collective-permute-start(bf16[64,1152]{1,0:T(8,128)(2,1)S(1)} %get-tuple-element.51), channel_id=1, source_target_pairs={{0,2},{1,3},{2,0},{3,1},{4,6},{5,7},{6,4},{7,5},{8,10},{9,11},{10,... | collective-permute-start | bytes 442376 | tf_op jit(solution)/shard_map/ppermute | solution.py:429
  66.2 1.7 %collective-permute-start.12 = (bf16[64,1152]{1,0:T(8,128)(2,1)S(1)}, bf16[64,1152]{1,0:T(8,128)(2,1)S(1)}, u32[]{:S(2)}, u32[]{:S(2)}) collective-permute-start(bf16[64,1152]{1,0:T(8,128)(2,1)S(1)} %get-tuple-element.41), channel_id=1, source_target_pairs={{0,1},{1,2},{2,3},{3,0},{4,5},{5,6},{6,7},{7,4},{8,9},{9,10},{10,1... | collective-permute-start | bytes 442376 | tf_op jit(solution)/shard_map/ppermute | solution.py:429
  67.8 0.9 collective-permute-start.13
  68.7 1.3 %collective-permute-done.18.refs_1_ = bf16[64,1152]{1,0:T(8,128)(2,1)S(1)} collective-permute-done((bf16[64,1152]{1,0:T(8,128)(2,1)S(1)}, bf16[64,1152]{1,0:T(8,128)(2,1)S(1)}, u32[]{:S(2)}, u32[]{:S(2)}) %collective-permute-start.18) | collective-permute-done | bytes 147488 | tf_op jit(solution)/shard_map/ppermute | solution.py:429
  70.0 3.5 %collective-permute-start.14 = (bf16[64,1152]{1,0:T(8,128)(2,1)S(1)}, bf16[64,1152]{1,0:T(8,128)(2,1)S(1)}, u32[]{:S(2)}, u32[]{:S(2)}) collective-permute-start(bf16[64,1152]{1,0:T(8,128)(2,1)S(1)} %get-tuple-element.43), channel_id=1, source_target_pairs={{0,3},{1,0},{2,1},{3,2},{4,7},{5,4},{6,5},{7,6},{8,11},{9,8},{10,9... | collective-permute-start | bytes 442376 | tf_op jit(solution)/shard_map/ppermute | solution.py:429
  73.4 3.4 %copy-done.5 = bf16[1024,4096]{1,0:T(8,128)(2,1)S(1)} copy-done((bf16[1024,4096]{1,0:T(8,128)(2,1)S(1)}, bf16[1024,4096]{1,0:T(8,128)(2,1)}, u32[]{:S(2)}) %copy-start.5) | copy-done | bytes 8388632
  77.4 3.0 %collective-permute-done.19.refs_2_ = bf16[64,1152]{1,0:T(8,128)(2,1)S(1)} collective-permute-done((bf16[64,1152]{1,0:T(8,128)(2,1)S(1)}, bf16[64,1152]{1,0:T(8,128)(2,1)S(1)}, u32[]{:S(2)}, u32[]{:S(2)}) %collective-permute-start.19) | collective-permute-done | bytes 147488 | tf_op jit(solution)/shard_map/ppermute | solution.py:429
  80.5 2.6 %project.3 = (bf16[64,1024]{1,0:T(8,128)(2,1)S(1)}, bf16[64,1024]{1,0:T(8,128)(2,1)S(1)}, bf16[64,1024]{1,0:T(8,128)(2,1)S(1)}, bf16[64,1024]{1,0:T(8,128)(2,1)S(1)}) custom-call(s32[4]{0:T(128)S(1)} %pad_add_fusion.1.order, bf16[64,1152]{1,0:T(8,128)(2,1)S(1)} %get-tuple-element.49.refs_0_, bf16[64,1152]{1,0:T(8,128)(2,1)S(1)} %collective-permute-done.18.refs_1_, ...), custom_call_target="tpu_custom_call" | custom-call | flops 536870912 | bytes 8388608 | tf_op jit(solution)/shard_map/project/pallas_call | solution.py:340
  83.3 1.8 %collective-permute-start.23 = (bf16[64,1024]{1,0:T(8,128)(2,1)S(1)}, bf16[64,1024]{1,0:T(8,128)(2,1)S(1)}, u32[]{:S(2)}, u32[]{:S(2)}) collective-permute-start(bf16[64,1024]{1,0:T(8,128)(2,1)S(1)} %get-tuple-element.56), channel_id=1, source_target_pairs={{0,12},{4,8},{8,4},{12,0},{1,13},{5,9},{9,5},{13,1},{2,14},{6,10},... | collective-permute-start | bytes 393224 | tf_op jit(solution)/shard_map/ppermute | solution.py:435
  85.0 2.8 %collective-permute-done.13.refs_2_ = bf16[64,1152]{1,0:T(8,128)(2,1)S(1)} collective-permute-done((bf16[64,1152]{1,0:T(8,128)(2,1)S(1)}, bf16[64,1152]{1,0:T(8,128)(2,1)S(1)}, u32[]{:S(2)}, u32[]{:S(2)}) %collective-permute-start.13) | collective-permute-done | bytes 147488 | tf_op jit(solution)/shard_map/ppermute | solution.py:429
  87.8 2.6 %project.2 = (bf16[64,1024]{1,0:T(8,128)(2,1)S(1)}, bf16[64,1024]{1,0:T(8,128)(2,1)S(1)}, bf16[64,1024]{1,0:T(8,128)(2,1)S(1)}, bf16[64,1024]{1,0:T(8,128)(2,1)S(1)}) custom-call(s32[4]{0:T(128)S(1)} %pad_add_fusion.1.order, bf16[64,1152]{1,0:T(8,128)(2,1)S(1)} %get-tuple-element.40.refs_0_, bf16[64,1152]{1,0:T(8,128)(2,1)S(1)} %collective-permute-done.12.refs_1_, ...), custom_call_target="tpu_custom_call" | custom-call | flops 536870912 | bytes 8388608 | tf_op jit(solution)/shard_map/project/pallas_call | solution.py:340
  90.5 1.8 %collective-permute-start.16 = (bf16[64,1024]{1,0:T(8,128)(2,1)S(1)}, bf16[64,1024]{1,0:T(8,128)(2,1)S(1)}, u32[]{:S(2)}, u32[]{:S(2)}) collective-permute-start(bf16[64,1024]{1,0:T(8,128)(2,1)S(1)} %get-tuple-element.47), channel_id=1, source_target_pairs={{0,8},{4,12},{8,0},{12,4},{1,9},{5,13},{9,1},{13,5},{2,10},{6,14},... | collective-permute-start | bytes 393224 | tf_op jit(solution)/shard_map/ppermute | solution.py:435
  92.4 4.6 %collective-permute-done.16.refs_2_ = bf16[64,1024]{1,0:T(8,128)(2,1)S(1)} collective-permute-done((bf16[64,1024]{1,0:T(8,128)(2,1)S(1)}, bf16[64,1024]{1,0:T(8,128)(2,1)S(1)}, u32[]{:S(2)}, u32[]{:S(2)}) %collective-permute-start.16) | collective-permute-done | bytes 131104 | tf_op jit(solution)/shard_map/ppermute | solution.py:435
  97.0 1.7 %collective-permute-done.17.refs_3_ = bf16[64,1024]{1,0:T(8,128)(2,1)S(1)} collective-permute-done((bf16[64,1024]{1,0:T(8,128)(2,1)S(1)}, bf16[64,1024]{1,0:T(8,128)(2,1)S(1)}, u32[]{:S(2)}, u32[]{:S(2)}) %collective-permute-start.17) | collective-permute-done | bytes 131104 | tf_op jit(solution)/shard_map/ppermute | solution.py:435
  98.7 0.9 sum_parts.1
  (56 shorter events, 4.5 us)
Async XLA Ops:
  0.0 7.9 %copy-start = (s32[4,4,1]{1,2,0:T(1,128)S(1)}, s32[4,4,1]{1,2,0:T(1,128)}, u32[]{:S(2)}) copy-start(s32[4,4,1]{1,2,0:T(1,128)} %param.15) | copy-start | bytes 196
  0.0 1.2 %copy-start.6 = (bf16[1,1,128,4096]{3,2,1,0:T(8,128)(2,1)S(1)}, bf16[1,1,128,4096]{3,2,1,0:T(8,128)(2,1)}, u32[]{:S(2)}) copy-start(bf16[1,1,128,4096]{3,2,1,0:T(8,128)(2,1)} %param.8) | copy-start | bytes 3145732
  2.5 29.3 %collective-permute-start.7 = (bf16[128,1280]{1,0:T(8,128)(2,1)S(1)}, bf16[128,1280]{1,0:T(8,128)(2,1)}, u32[]{:S(2)}, u32[]{:S(2)}) collective-permute-start(bf16[128,1280]{1,0:T(8,128)(2,1)S(1)} %get-tuple-element.33), channel_id=1, source_target_pairs={{0,8},{4,12},{8,0},{12,4},{1,9},{5,13},{9,1},{13,5},{2,10},{6,14},... | collective-permute-start | bytes 983048 | tf_op jit(solution)/shard_map/ppermute | solution.py:373
  5.5 37.6 %collective-permute-start.6 = (bf16[128,1280]{1,0:T(8,128)(2,1)S(1)}, bf16[128,1280]{1,0:T(8,128)(2,1)}, u32[]{:S(2)}, u32[]{:S(2)}) collective-permute-start(bf16[128,1280]{1,0:T(8,128)(2,1)S(1)} %get-tuple-element.33), channel_id=1, source_target_pairs={{0,4},{4,0},{8,12},{12,8},{1,5},{5,1},{9,13},{13,9},{2,6},{6,2},{1... | collective-permute-start | bytes 983048 | tf_op jit(solution)/shard_map/ppermute | solution.py:376
  5.5 19.8 %collective-permute-start.4 = (bf16[128,2048]{1,0:T(8,128)(2,1)S(1)}, bf16[128,2048]{1,0:T(8,128)(2,1)S(1)}, u32[]{:S(2)}, u32[]{:S(2)}) collective-permute-start(bf16[128,2048]{1,0:T(8,128)(2,1)S(1)} %get-tuple-element.31), channel_id=1, source_target_pairs={{0,8},{4,12},{8,0},{12,4},{1,9},{5,13},{9,1},{13,5},{2,10},{6,14},... | collective-permute-start | bytes 1572872 | tf_op jit(solution)/shard_map/ppermute | solution.py:373
  5.7 28.8 %collective-permute-start.3 = (bf16[128,2048]{1,0:T(8,128)(2,1)S(1)}, bf16[128,2048]{1,0:T(8,128)(2,1)S(1)}, u32[]{:S(2)}, u32[]{:S(2)}) collective-permute-start(bf16[128,2048]{1,0:T(8,128)(2,1)S(1)} %get-tuple-element.31), channel_id=1, source_target_pairs={{0,4},{4,0},{8,12},{12,8},{1,5},{5,1},{9,13},{13,9},{2,6},{6,2},{1... | collective-permute-start | bytes 1572872 | tf_op jit(solution)/shard_map/ppermute | solution.py:376
  6.0 33.1 %collective-permute-start.10 = (bf16[128,768]{1,0:T(8,128)(2,1)S(1)}, bf16[128,768]{1,0:T(8,128)(2,1)S(1)}, u32[]{:S(2)}, u32[]{:S(2)}) collective-permute-start(bf16[128,768]{1,0:T(8,128)(2,1)S(1)} %get-tuple-element.36), channel_id=1, source_target_pairs={{0,8},{4,12},{8,0},{12,4},{1,9},{5,13},{9,1},{13,5},{2,10},{6,14},... | collective-permute-start | bytes 589832 | tf_op jit(solution)/shard_map/ppermute | solution.py:373
  8.6 5.8 %copy-start.3 = (bf16[4096,2,1024]{2,1,0:T(2,128)(2,1)S(1)}, bf16[4096,2,1024]{2,1,0:T(2,128)(2,1)}, u32[]{:S(2)}) copy-start(bf16[4096,2,1024]{2,1,0:T(2,128)(2,1)} %src.1) | copy-start | bytes 50331652
  14.4 10.9 %copy-start.2 = (bf16[2,64,4096]{2,1,0:T(8,128)(2,1)S(1)}, bf16[2,64,4096]{2,1,0:T(8,128)(2,1)}, u32[]{:S(2)}) copy-start(bf16[2,64,4096]{2,1,0:T(8,128)(2,1)} %res_ref.1) | copy-start | bytes 3145732
  14.4 10.9 %copy-start.8 = (bf16[4096]{0:T(1024)(128)(2,1)S(1)}, bf16[4096]{0:T(1024)(128)(2,1)}, u32[]{:S(2)}) copy-start(bf16[4096]{0:T(1024)(128)(2,1)} %param.11) | copy-start | bytes 24580
  25.3 7.1 %collective-permute-start.5 = (bf16[128,2048]{1,0:T(8,128)(2,1)S(1)}, bf16[128,2048]{1,0:T(8,128)(2,1)S(1)}, u32[]{:S(2)}, u32[]{:S(2)}) collective-permute-start(bf16[128,2048]{1,0:T(8,128)(2,1)S(1)} %collective-permute-done.4), channel_id=1, source_target_pairs={{0,4},{4,0},{8,12},{12,8},{1,5},{5,1},{9,13},{13,9},{2,6},{6,2},{1... | collective-permute-start | bytes 1572872 | tf_op jit(solution)/shard_map/ppermute | solution.py:376
  25.4 3.4 %copy-start.4 = (bf16[4096,1024]{1,0:T(8,128)(2,1)S(1)}, bf16[4096,1024]{1,0:T(8,128)(2,1)}, u32[]{:S(2)}) copy-start(bf16[4096,1024]{1,0:T(8,128)(2,1)} %w_hbm.1) | copy-start | bytes 25165828
  31.8 15.4 %collective-permute-start.9 = (bf16[128,768]{1,0:T(8,128)(2,1)S(1)}, bf16[128,768]{1,0:T(8,128)(2,1)S(1)}, u32[]{:S(2)}, u32[]{:S(2)}) collective-permute-start(bf16[128,768]{1,0:T(8,128)(2,1)S(1)} %get-tuple-element.36), channel_id=1, source_target_pairs={{0,4},{4,0},{8,12},{12,8},{1,5},{5,1},{9,13},{13,9},{2,6},{6,2},{1... | collective-permute-start | bytes 589832 | tf_op jit(solution)/shard_map/ppermute | solution.py:376
  32.4 17.1 %collective-permute-start = (bf16[128,1024]{1,0:T(8,128)(2,1)S(1)}, bf16[128,1024]{1,0:T(8,128)(2,1)S(1)}, u32[]{:S(2)}, u32[]{:S(2)}) collective-permute-start(bf16[128,1024]{1,0:T(8,128)(2,1)S(1)} %query_rows.1.refs_0_), channel_id=1, source_target_pairs={{0,1},{1,2},{2,3},{3,0},{4,5},{5,6},{6,7},{7,4},{8,9},{9,10},{10,1... | collective-permute-start | bytes 786440 | tf_op jit(solution)/shard_map/ppermute | solution.py:386
  34.5 7.3 %collective-permute-start.8 = (bf16[128,1280]{1,0:T(8,128)(2,1)}, bf16[128,1280]{1,0:T(8,128)(2,1)S(1)}, u32[]{:S(2)}, u32[]{:S(2)}) collective-permute-start(bf16[128,1280]{1,0:T(8,128)(2,1)} %collective-permute-done.7), channel_id=1, source_target_pairs={{0,4},{4,0},{8,12},{12,8},{1,5},{5,1},{9,13},{13,9},{2,6},{6,2},{1... | collective-permute-start | bytes 983048 | tf_op jit(solution)/shard_map/ppermute | solution.py:376
  39.1 15.8 %collective-permute-start.1 = (bf16[128,1024]{1,0:T(8,128)(2,1)S(1)}, bf16[128,1024]{1,0:T(8,128)(2,1)S(1)}, u32[]{:S(2)}, u32[]{:S(2)}) collective-permute-start(bf16[128,1024]{1,0:T(8,128)(2,1)S(1)} %query_rows.1.refs_0_), channel_id=1, source_target_pairs={{0,2},{1,3},{2,0},{3,1},{4,6},{5,7},{6,4},{7,5},{8,10},{9,11},{10,... | collective-permute-start | bytes 786440 | tf_op jit(solution)/shard_map/ppermute | solution.py:386
  41.8 13.1 %collective-permute-start.2 = (bf16[128,1024]{1,0:T(8,128)(2,1)S(1)}, bf16[128,1024]{1,0:T(8,128)(2,1)S(1)}, u32[]{:S(2)}, u32[]{:S(2)}) collective-permute-start(bf16[128,1024]{1,0:T(8,128)(2,1)S(1)} %query_rows.1.refs_0_), channel_id=1, source_target_pairs={{0,3},{1,0},{2,1},{3,2},{4,7},{5,4},{6,5},{7,6},{8,11},{9,8},{10,9... | collective-permute-start | bytes 786440 | tf_op jit(solution)/shard_map/ppermute | solution.py:386
  43.1 4.1 %collective-permute-start.11 = (bf16[128,768]{1,0:T(8,128)(2,1)S(1)}, bf16[128,768]{1,0:T(8,128)(2,1)S(1)}, u32[]{:S(2)}, u32[]{:S(2)}) collective-permute-start(bf16[128,768]{1,0:T(8,128)(2,1)S(1)} %collective-permute-done.10), channel_id=1, source_target_pairs={{0,4},{4,0},{8,12},{12,8},{1,5},{5,1},{9,13},{13,9},{2,6},{6,2},{1... | collective-permute-start | bytes 589832 | tf_op jit(solution)/shard_map/ppermute | solution.py:376
  57.9 12.0 %collective-permute-start.18 = (bf16[64,1152]{1,0:T(8,128)(2,1)S(1)}, bf16[64,1152]{1,0:T(8,128)(2,1)S(1)}, u32[]{:S(2)}, u32[]{:S(2)}) collective-permute-start(bf16[64,1152]{1,0:T(8,128)(2,1)S(1)} %get-tuple-element.50), channel_id=1, source_target_pairs={{0,1},{1,2},{2,3},{3,0},{4,5},{5,6},{6,7},{7,4},{8,9},{9,10},{10,1... | collective-permute-start | bytes 442376 | tf_op jit(solution)/shard_map/ppermute | solution.py:429
  63.7 16.7 %collective-permute-start.19 = (bf16[64,1152]{1,0:T(8,128)(2,1)S(1)}, bf16[64,1152]{1,0:T(8,128)(2,1)S(1)}, u32[]{:S(2)}, u32[]{:S(2)}) collective-permute-start(bf16[64,1152]{1,0:T(8,128)(2,1)S(1)} %get-tuple-element.51), channel_id=1, source_target_pairs={{0,2},{1,3},{2,0},{3,1},{4,6},{5,7},{6,4},{7,5},{8,10},{9,11},{10,... | collective-permute-start | bytes 442376 | tf_op jit(solution)/shard_map/ppermute | solution.py:429
  65.8 14.7 %collective-permute-start.20 = (bf16[64,1152]{1,0:T(8,128)(2,1)S(1)}, bf16[64,1152]{1,0:T(8,128)(2,1)S(1)}, u32[]{:S(2)}, u32[]{:S(2)}) collective-permute-start(bf16[64,1152]{1,0:T(8,128)(2,1)S(1)} %get-tuple-element.52), channel_id=1, source_target_pairs={{0,3},{1,0},{2,1},{3,2},{4,7},{5,4},{6,5},{7,6},{8,11},{9,8},{10,9... | collective-permute-start | bytes 442376 | tf_op jit(solution)/shard_map/ppermute | solution.py:429
  66.2 17.1 %collective-permute-start.12 = (bf16[64,1152]{1,0:T(8,128)(2,1)S(1)}, bf16[64,1152]{1,0:T(8,128)(2,1)S(1)}, u32[]{:S(2)}, u32[]{:S(2)}) collective-permute-start(bf16[64,1152]{1,0:T(8,128)(2,1)S(1)} %get-tuple-element.41), channel_id=1, source_target_pairs={{0,1},{1,2},{2,3},{3,0},{4,5},{5,6},{6,7},{7,4},{8,9},{9,10},{10,1... | collective-permute-start | bytes 442376 | tf_op jit(solution)/shard_map/ppermute | solution.py:429
  67.8 20.0 %collective-permute-start.13 = (bf16[64,1152]{1,0:T(8,128)(2,1)S(1)}, bf16[64,1152]{1,0:T(8,128)(2,1)S(1)}, u32[]{:S(2)}, u32[]{:S(2)}) collective-permute-start(bf16[64,1152]{1,0:T(8,128)(2,1)S(1)} %get-tuple-element.42), channel_id=1, source_target_pairs={{0,2},{1,3},{2,0},{3,1},{4,6},{5,7},{6,4},{7,5},{8,10},{9,11},{10,... | collective-permute-start | bytes 442376 | tf_op jit(solution)/shard_map/ppermute | solution.py:429
  70.0 17.9 %collective-permute-start.14 = (bf16[64,1152]{1,0:T(8,128)(2,1)S(1)}, bf16[64,1152]{1,0:T(8,128)(2,1)S(1)}, u32[]{:S(2)}, u32[]{:S(2)}) collective-permute-start(bf16[64,1152]{1,0:T(8,128)(2,1)S(1)} %get-tuple-element.43), channel_id=1, source_target_pairs={{0,3},{1,0},{2,1},{3,2},{4,7},{5,4},{6,5},{7,6},{8,11},{9,8},{10,9... | collective-permute-start | bytes 442376 | tf_op jit(solution)/shard_map/ppermute | solution.py:429
  73.4 3.4 %copy-start.5 = (bf16[1024,4096]{1,0:T(8,128)(2,1)S(1)}, bf16[1024,4096]{1,0:T(8,128)(2,1)}, u32[]{:S(2)}) copy-start(bf16[1024,4096]{1,0:T(8,128)(2,1)} %src.2) | copy-start | bytes 25165828
  83.1 9.3 %collective-permute-start.21 = (bf16[64,1024]{1,0:T(8,128)(2,1)S(1)}, bf16[64,1024]{1,0:T(8,128)(2,1)S(1)}, u32[]{:S(2)}, u32[]{:S(2)}) collective-permute-start(bf16[64,1024]{1,0:T(8,128)(2,1)S(1)} %get-tuple-element.54), channel_id=1, source_target_pairs={{0,4},{4,0},{8,12},{12,8},{1,5},{5,1},{9,13},{13,9},{2,6},{6,2},{1... | collective-permute-start | bytes 393224 | tf_op jit(solution)/shard_map/ppermute | solution.py:435
  83.2 9.2 %collective-permute-start.22 = (bf16[64,1024]{1,0:T(8,128)(2,1)S(1)}, bf16[64,1024]{1,0:T(8,128)(2,1)S(1)}, u32[]{:S(2)}, u32[]{:S(2)}) collective-permute-start(bf16[64,1024]{1,0:T(8,128)(2,1)S(1)} %get-tuple-element.55), channel_id=1, source_target_pairs={{0,8},{4,12},{8,0},{12,4},{1,9},{5,13},{9,1},{13,5},{2,10},{6,14},... | collective-permute-start | bytes 393224 | tf_op jit(solution)/shard_map/ppermute | solution.py:435
  83.3 9.1 %collective-permute-start.23 = (bf16[64,1024]{1,0:T(8,128)(2,1)S(1)}, bf16[64,1024]{1,0:T(8,128)(2,1)S(1)}, u32[]{:S(2)}, u32[]{:S(2)}) collective-permute-start(bf16[64,1024]{1,0:T(8,128)(2,1)S(1)} %get-tuple-element.56), channel_id=1, source_target_pairs={{0,12},{4,8},{8,4},{12,0},{1,13},{5,9},{9,5},{13,1},{2,14},{6,10},... | collective-permute-start | bytes 393224 | tf_op jit(solution)/shard_map/ppermute | solution.py:435
  87.8 11.7 %copy-start.1 = (s32[4,4,1]{1,2,0:T(1,128)S(1)}, s32[4,4,1]{1,2,0:T(1,128)}, u32[]{:S(2)}) copy-start(s32[4,4,1]{1,2,0:T(1,128)} %param.15) | copy-start | bytes 196
  90.5 1.9 %collective-permute-start.15 = (bf16[64,1024]{1,0:T(8,128)(2,1)S(1)}, bf16[64,1024]{1,0:T(8,128)(2,1)S(1)}, u32[]{:S(2)}, u32[]{:S(2)}) collective-permute-start(bf16[64,1024]{1,0:T(8,128)(2,1)S(1)} %get-tuple-element.46), channel_id=1, source_target_pairs={{0,4},{4,0},{8,12},{12,8},{1,5},{5,1},{9,13},{13,9},{2,6},{6,2},{1... | collective-permute-start | bytes 393224 | tf_op jit(solution)/shard_map/ppermute | solution.py:435
  90.5 6.4 %collective-permute-start.16 = (bf16[64,1024]{1,0:T(8,128)(2,1)S(1)}, bf16[64,1024]{1,0:T(8,128)(2,1)S(1)}, u32[]{:S(2)}, u32[]{:S(2)}) collective-permute-start(bf16[64,1024]{1,0:T(8,128)(2,1)S(1)} %get-tuple-element.47), channel_id=1, source_target_pairs={{0,8},{4,12},{8,0},{12,4},{1,9},{5,13},{9,1},{13,5},{2,10},{6,14},... | collective-permute-start | bytes 393224 | tf_op jit(solution)/shard_map/ppermute | solution.py:435
  92.3 6.4 %collective-permute-start.17 = (bf16[64,1024]{1,0:T(8,128)(2,1)S(1)}, bf16[64,1024]{1,0:T(8,128)(2,1)S(1)}, u32[]{:S(2)}, u32[]{:S(2)}) collective-permute-start(bf16[64,1024]{1,0:T(8,128)(2,1)S(1)} %get-tuple-element.48), channel_id=1, source_target_pairs={{0,12},{4,8},{8,4},{12,0},{1,13},{5,9},{9,5},{13,1},{2,14},{6,10},... | collective-permute-start | bytes 393224 | tf_op jit(solution)/shard_map/ppermute | solution.py:435
  (1 other events, 0.7 us)
where the time goes:
time: 101 us; the launch traced here: 99.6 us
  starting transfers between devices  30 us (30%)
  waiting for transfers between devices  28.7 us (28%)
  local copies, waits for them, and re-layouts  15.1 us (15%)
  Pallas kernels  14.4 us (14%)
  matrix products  10.9 us (11%)
    unnamed x18, local copies, waits for them, and re-layouts  14.5 us
    ppermute x6, starting transfers between devices, body(): lax.ppermute(sent[hop * per + j], 'qset', set_move(hop))  14.2 us
    dot_general x3, matrix products, body(): jnp.einsum('rd,dkc->rkc', jnp.concatenate(chunks, axis=0), weight, prefer...  10.9 us
    ppermute x3, waiting for transfers between devices, cross(): lax.ppermute(own, 'seq', seq_move(hop, 0))  9.74 us
    ppermute x6, waiting for transfers between devices, body(): lax.ppermute(sent[hop * per + j], 'qset', set_move(hop))  7.11 us
    ppermute x6, waiting for transfers between devices, body(): lax.ppermute(out[i], 'seq', seq_move(*moves[i]))  6.31 us
    ppermute x3, starting transfers between devices, body(): lax.ppermute(queries, 'qset', set_move(hop))  6.1 us
    ppermute x3, waiting for transfers between devices, body(): lax.ppermute(queries, 'qset', set_move(hop))  5.5 us
  transfers between devices with their start and end apart: 24, of which 7 were waited for; matrix products, arithmetic and copies ran while one was open for 12% of the time, Pallas kernels for 10%

commit v1 on v0

--- a/solution.py
+++ b/solution.py
@@ -12,7 +12,7 @@
 EPSILON = 1e-06
 EMPTY = -1e30
 LANES = 128
-CUTS = (0, 8, 13, 16)
+CUTS = (0, 7, 12, 16)
 
 
 F32 = jnp.float32
@@ -176,13 +176,34 @@
     return hi, mid, low
 
 
-def attend_kernel(n_pass, plen, heads, dests, table, *refs):
+def fill_table(question_ref, table, n_pass, per, n_set):
+    chips = n_pass // 2
+    me_set, me_seq = lax.axis_index("qset"), lax.axis_index("seq")
+    chip = lax.div(me_seq, 2)
+    core = me_seq - 2 * chip
+    for t in range(n_set * per):
+        table[1, t] = -1
+        table[2, t] = -1
+    for i in range(n_pass):
+        hop, flip = divmod(i, 2)
+        source = 2 * lax.rem(chip + chips - hop, chips) + (1 - core if flip else core)
+        question = question_ref[me_set, source]
+        owner = lax.div(question, per)
+        number = question - owner * per
+        table[0, i] = lax.rem(me_set + n_set - owner, n_set) * per + number
+        t = lax.rem(owner + n_set - me_set, n_set) * per + number
+        row = jnp.where(table[1, t] < 0, 1, 2)
+        table[row, t] = i
+
+
+def attend_kernel(n_pass, plen, heads, dests, question_ref, *refs):
     q_refs = refs[:dests]
     kv_ref = refs[dests]
-    out_refs = refs[dests + 1 : -7]
-    qs, score_s, weight_s, part, peak_s, total_s, stat_s = refs[-7:]
+    out_refs = refs[dests + 1 : -9]
+    qs, score_s, weight_s, part, peak_s, total_s, stat_s, sent_s, table = refs[-9:]
     dec_len, cols = out_refs[0].shape[0], heads * HD
     per = len(out_refs) // dests
+    fill_table(question_ref, table, n_pass, per, dests)
     wide = score_s.shape[1] // dec_len
     span_w = wide * HD
     groups = cols // span_w
@@ -239,28 +260,19 @@
         )
         part[p, :, span] = pick(summed)
 
-    def put_stats(out, peaks, totals):
-        p_hi, p_mid, p_low = split3(peaks)
-        t_hi, t_low, _ = split3(totals)
-        packed = jnp.concatenate(
-            [v[:, :heads] for v in (p_hi, p_mid, p_low, t_hi, t_low)]
-            + [jnp.zeros((dec_len, LANES - 5 * heads), BF16)],
-            axis=1,
-        )
-        out[:, cols:] = packed
-
     for t, out in enumerate(out_refs):
         a, b = table[1, t], table[2, t]
 
         @pl.when(a < 0)
         def _():
             out[:, :cols] = jnp.zeros((dec_len, cols), BF16)
-            put_stats(out, jnp.full((dec_len, LANES), EMPTY, F32), jnp.zeros((dec_len, LANES), F32))
+            sent_s[t, 0] = jnp.full((dec_len, LANES), EMPTY, F32)
+            sent_s[t, 1] = jnp.zeros((dec_len, LANES), F32)
 
         @pl.when((a >= 0) & (b < 0))
         def _():
             out[:, :cols] = (part[a] / total_s[a]).astype(BF16)
-            put_stats(out, stat_s[a, 0], stat_s[a, 1])
+            sent_s[t] = stat_s[a]
 
         @pl.when((a >= 0) & (b >= 0))
         def _():
@@ -269,24 +281,38 @@
             whole = total_s[a] * f_a + total_s[b] * f_b
             out[:, :cols] = ((part[a] * f_a + part[b] * f_b) / whole).astype(BF16)
             peaks = jnp.maximum(stat_s[a, 0], stat_s[b, 0])
-            totals = stat_s[a, 1] * jnp.exp(stat_s[a, 0] - peaks) + stat_s[b, 1] * jnp.exp(
+            sent_s[t, 0] = peaks
+            sent_s[t, 1] = stat_s[a, 1] * jnp.exp(stat_s[a, 0] - peaks) + stat_s[b, 1] * jnp.exp(
                 stat_s[b, 0] - peaks
             )
-            put_stats(out, peaks, totals)
-
-
-def attend(table, queries, kv, n_pass, plen, per, dec_len):
+
+    for r in range(dests):
+        pieces = []
+        for t in range(r * per, (r + 1) * per):
+            for piece in (*split3(sent_s[t, 0]), sent_s[t, 1].astype(BF16)):
+                pieces.append(piece[:, :heads])
+        room = out_refs[r * per].shape[1] - cols - 4 * heads * per
+        if room:
+            pieces.append(jnp.zeros((dec_len, room), BF16))
+        out_refs[r * per][:, cols:] = jnp.concatenate(pieces, axis=1)
+
+
+def attend(questions, queries, kv, n_pass, plen, per, dec_len):
     dests = len(queries)
     cols = queries[0].shape[1]
     heads = cols // HD
     rows = n_pass * dec_len
     wide = min(heads, 4)
     units = n_pass * heads // wide
+    extra = -(-4 * heads * per // LANES) * LANES
     return pl.pallas_call(
         functools.partial(attend_kernel, n_pass, plen, heads, dests),
         in_specs=[pl.BlockSpec(memory_space=pltpu.SMEM)] + [full_spec()] * (dests + 1),
         out_specs=[full_spec()] * (dests * per),
-        out_shape=[jax.ShapeDtypeStruct((dec_len, cols + LANES), BF16)] * (dests * per),
+        out_shape=[
+            jax.ShapeDtypeStruct((dec_len, cols if t % per else cols + extra), BF16)
+            for t in range(dests * per)
+        ],
         scratch_shapes=[
             pltpu.VMEM((dests * per, dec_len, cols), BF16),
             pltpu.VMEM((units, wide * dec_len, plen), F32),
@@ -295,25 +321,26 @@
             pltpu.VMEM((n_pass, dec_len, cols), F32),
             pltpu.VMEM((n_pass, dec_len, cols), F32),
             pltpu.VMEM((n_pass, 2, dec_len, LANES), F32),
+            pltpu.VMEM((dests * per, 2, dec_len, LANES), F32),
+            pltpu.SMEM((3, max(n_pass, dests * per)), jnp.int32),
         ],
         cost_estimate=cost(8 * rows * plen * cols, n_pass * plen * cols * 4),
         compiler_params=pltpu.CompilerParams(vmem_limit_bytes=20 << 20),
         name="attend",
-    )(table, *queries, kv)
-
-
-def project_kernel(heads, parts, order, *refs):
-    part_refs = refs[:parts]
-    w_ref = refs[parts]
-    out_refs = refs[parts + 1 : -1]
-    rows_ref = refs[-1]
+    )(questions, *queries, kv)
+
+
+def project_kernel(heads, parts, number, *refs):
+    part_refs, stat_refs = refs[:parts], refs[parts : 2 * parts]
+    w_ref = refs[2 * parts]
+    out_refs, rows_ref = refs[2 * parts + 1 : -1], refs[-1]
     dec_len, cols = part_refs[0].shape[0], heads * HD
-    row = lax.broadcasted_iota(jnp.int32, (LANES, cols), 0)
-    head = lax.broadcasted_iota(jnp.int32, (LANES, cols), 1) // HD
-    same = (row % heads == head).astype(F32)
-    spread_peak = jnp.where(row < 3 * heads, same, 0.0).astype(BF16)
-    spread_total = jnp.where((row >= 3 * heads) & (row < 5 * heads), same, 0.0).astype(BF16)
-    stats = jnp.concatenate([ref[:, cols:] for ref in part_refs], axis=0)
+    stats = jnp.concatenate([ref[:, cols:] for ref in stat_refs], axis=0)
+    row = lax.broadcasted_iota(jnp.int32, (stats.shape[1], cols), 0) - number * 4 * heads
+    head = lax.broadcasted_iota(jnp.int32, (stats.shape[1], cols), 1) // HD
+    is_peak = functools.reduce(jnp.logical_or, [row == head + i * heads for i in range(3)])
+    spread_peak = is_peak.astype(F32).astype(BF16)
+    spread_total = (row == head + 3 * heads).astype(F32).astype(BF16)
     peaks = jnp.dot(stats, spread_peak, preferred_element_type=F32)
     totals = jnp.dot(stats, spread_total, preferred_element_type=F32)
     peaks = [peaks[i * dec_len : (i + 1) * dec_len] for i in range(parts)]
@@ -325,28 +352,32 @@
     )
     rows_ref[...] = (mixed / functools.reduce(jnp.add, sizes)).astype(BF16)
     piece = out_refs[0].shape[1]
+    chips = len(out_refs) // 2
+    me_seq = lax.axis_index("seq")
+    chip = lax.div(me_seq, 2)
+    core = me_seq - 2 * chip
     for i, out in enumerate(out_refs):
-        cut = pl.ds(pl.multiple_of(order[i] * piece, piece), piece)
+        hop, flip = divmod(i, 2)
+        dest = 2 * lax.rem(chip + hop, chips) + (1 - core if flip else core)
+        cut = pl.ds(pl.multiple_of(dest * piece, piece), piece)
         out[...] = jnp.dot(rows_ref[...], w_ref[:, cut], preferred_element_type=F32).astype(BF16)
 
 
-def project(order, partials, weight):
+def project(number, partials, stats, weight, count):
     parts = len(partials)
-    rows, wide = partials[0].shape
-    cols = wide - LANES
-    heads = cols // HD
-    count = order.shape[0]
+    rows = partials[0].shape[0]
+    cols = weight.shape[0]
     piece = weight.shape[1] // count
     return pl.pallas_call(
-        functools.partial(project_kernel, heads, parts),
-        in_specs=[pl.BlockSpec(memory_space=pltpu.SMEM)] + [full_spec()] * (parts + 1),
+        functools.partial(project_kernel, cols // HD, parts, number),
+        in_specs=[full_spec()] * (2 * parts + 1),
         out_specs=[full_spec()] * count,
         out_shape=[jax.ShapeDtypeStruct((rows, piece), BF16)] * count,
         scratch_shapes=[pltpu.VMEM((rows, cols), BF16)],
         cost_estimate=cost(2 * rows * cols * weight.shape[1], cols * weight.shape[1] * 2),
         compiler_params=pltpu.CompilerParams(vmem_limit_bytes=16 << 20),
         name="project",
-    )(order, *partials, weight)
+    )(*partials, *stats, weight)
 
 
 def body(
@@ -356,11 +387,9 @@
     plen = states.shape[2]
     n_set = lax.axis_size("qset")
     n_seq = lax.axis_size("seq")
-    me_set = lax.axis_index("qset")
     me_seq = lax.axis_index("seq")
     per, dec_len = dec_states.shape[0], dec_states.shape[1]
     chips = n_seq // 2
-    chip, core = me_seq // 2, me_seq % 2
     cuts = [width * c // 16 for c in CUTS]
 
     def seq_move(hop, flip):
@@ -378,33 +407,14 @@
     own = list(enc_norm(states[0, 0], enc_gain, cuts))
     queries = query_rows(dec_states.reshape(per * dec_len, width), dec_gain, query_weight)
     crossed = [cross(rows) for rows in own]
-    slot_seq = jnp.stack(
-        [2 * ((chip - hop) % chips) + (core ^ f) for hop in range(chips) for f in range(2)]
-    )
-
     all_queries = [queries] + [
         lax.ppermute(queries, "qset", set_move(hop)) for hop in range(1, n_set)
     ]
 
-    passages = lax.dynamic_index_in_dim(question_of[:, :, 0], me_set, 0, keepdims=False)
-    passages = passages[slot_seq]
-    owner, number = passages // per, passages % per
-    query_slot = ((me_set - owner) % n_set) * per + number
-    out_slot = ((owner - me_set) % n_set) * per + number
-    index = jnp.arange(n_seq, dtype=jnp.int32)
-    named = out_slot[None, :] == jnp.arange(n_set * per, dtype=jnp.int32)[:, None]
-    high = jnp.max(jnp.where(named, index[None, :], -1), axis=1)
-    low = jnp.min(jnp.where(named, index[None, :], n_seq), axis=1)
-    first = jnp.where(high >= 0, low, -1)
-    second = jnp.where(high > low, high, -1)
-    size = max(n_seq, n_set * per)
-    table = jnp.stack([jnp.pad(v, (0, size - v.shape[0])) for v in (query_slot, first, second)])
-
-    kv_parts = load(key_value_weight, cuts, 4096, 20 << 20)
-    acc, forwarded = None, ()
+    kv_parts = load(key_value_weight, cuts, 256, 28 << 20)
+    acc = None
     for c, weight in enumerate(kv_parts):
-        beside = sibling(own[c])
-        here, _ = lax.optimization_barrier((crossed[c], (forwarded, acc if c > 1 else ())))
+        beside, here = sibling(own[c]), crossed[c]
         forwarded = [sibling(rows) for rows in here]
         chunks = [own[c], beside]
         for pair in zip(here, forwarded):
@@ -415,12 +425,10 @@
         acc = part if acc is None else acc + part
     kv = jnp.transpose(acc.astype(BF16), (1, 0, 2))
 
-    sent = list(attend(table, all_queries, kv, n_seq, plen, per, dec_len))
+    sent = list(attend(question_of[:, :, 0], all_queries, kv, n_seq, plen, per, dec_len))
     out_source, sent[0] = lax.optimization_barrier((out_weight, sent[0]))
-    (out_part,) = load(out_source, [0, out_weight.shape[0]], 256, 20 << 20)
+    (out_part,) = load(out_source, [0, out_weight.shape[0]], 256, 42 << 20)
     moves = [(hop, f) for hop in range(chips) for f in range(2)]
-    order = jnp.stack([2 * ((chip + hop) % chips) + (core ^ f) for hop, f in moves])
-    order = order.astype(jnp.int32)
 
     partials = []
     for j in range(per):
@@ -430,7 +438,7 @@
         )
     parts = []
     for j in range(per):
-        out = project(order, partials[j], out_part)
+        out = project(j, partials[j], partials[0], out_part, n_seq)
         parts += [out[0]] + [
             lax.ppermute(out[i], "seq", seq_move(*moves[i])) for i in range(1, len(moves))
         ]

time: 101 us -> 95 us (0.941)
  local copies, waits for them, and re-layouts: 15.1 us -> 1.95 us
  Pallas kernels: 14.4 us -> 20.8 us
  matrix products: 10.9 us -> 13.7 us
    unnamed x18, local copies, waits for them, and re-layouts: 14.5 us -> 1.95 us
    pallas_call x2, Pallas kernels: 1.74 us -> 9.43 us  [load(): pl.pallas_call(functools.partial(load_kernel, cuts, step), in_specs=[pl.B...]
    ppermute x6, waiting for transfers between devices: 7.11 us -> 11.8 us  [body(): lax.ppermute(sent[hop * per + j], 'qset', set_move(hop))]
    ppermute x3, waiting for transfers between devices: 5.5 us -> 1.95 us  [body(): lax.ppermute(queries, 'qset', set_move(hop))]
    ppermute x3, waiting for transfers between devices: 9.74 us -> 6.42 us  [cross(): lax.ppermute(own, 'seq', seq_move(hop, 0))]
    dot_general x3, matrix products: 10.9 us -> 13.7 us  [body(): jnp.einsum('rd,dkc->rkc', jnp.concatenate(chunks, axis=0), weight, prefer...]
    ppermute x6, waiting for transfers between devices: 6.31 us -> 7.98 us  [body(): lax.ppermute(out[i], 'seq', seq_move(*moves[i]))]
    pallas_call x2, Pallas kernels: 5.25 us -> 4.05 us  [project(): pl.pallas_call(functools.partial(project_kernel, cols // HD, parts, numbe...]
  transfers between devices with their start and end apart: 24 -> 24, of which waited for: 7 -> 9; matrix products, arithmetic and copies ran while one was open for 12% -> 15% of each run, Pallas kernels for 10% -> 15%
where the time goes in v1:
time: 95 us; the launch traced here: 94 us
  starting transfers between devices  29.2 us (31%)
  waiting for transfers between devices  28.1 us (30%)
  Pallas kernels  20.8 us (22%)
  matrix products  13.7 us (14%)
  local copies, waits for them, and re-layouts  1.95 us (2%)
    dot_general x3, matrix products, body(): jnp.einsum('rd,dkc->rkc', jnp.concatenate(chunks, axis=0), weight, prefer...  13.7 us
    ppermute x6, starting transfers between devices, body(): lax.ppermute(sent[hop * per + j], 'qset', set_move(hop))  13.3 us
    ppermute x6, waiting for transfers between devices, body(): lax.ppermute(sent[hop * per + j], 'qset', set_move(hop))  11.8 us
    pallas_call x2, Pallas kernels, load(): pl.pallas_call(functools.partial(load_kernel, cuts, step), in_specs=[pl.B...  9.43 us
    ppermute x6, waiting for transfers between devices, body(): lax.ppermute(out[i], 'seq', seq_move(*moves[i]))  7.98 us
    ppermute x3, waiting for transfers between devices, cross(): lax.ppermute(own, 'seq', seq_move(hop, 0))  6.42 us
    ppermute x3, starting transfers between devices, body(): lax.ppermute(queries, 'qset', set_move(hop))  6.11 us
    ppermute x3, starting transfers between devices, cross(): lax.ppermute(own, 'seq', seq_move(hop, 0))  4.99 us
  transfers between devices with their start and end apart: 24, of which 9 were waited for; matrix products, arithmetic and copies ran while one was open for 15% of the time, Pallas kernels for 15%

profile of v1, /device:TPU:0, one launch (start us, length us, event | category | flops | bytes accessed | tf_op | source)
XLA Modules:
  0.0 94.0 jit_solution(9229703184389983715)
XLA Ops:
  0.0 1.2 %copy-done.2 = bf16[1,1,128,4096]{3,2,1,0:T(8,128)(2,1)S(1)} copy-done((bf16[1,1,128,4096]{3,2,1,0:T(8,128)(2,1)S(1)}, bf16[1,1,128,4096]{3,2,1,0:T(8,128)(2,1)}, u32[]{:S(2)}) %copy-start.2) | copy-done | bytes 1048600
  1.2 0.7 copy-done.3
  2.4 3.0 %collective-permute-start.7 = (bf16[128,1280]{1,0:T(8,128)(2,1)S(1)}, bf16[128,1280]{1,0:T(8,128)(2,1)S(1)}, u32[]{:S(2)}, u32[]{:S(2)}) collective-permute-start(bf16[128,1280]{1,0:T(8,128)(2,1)S(1)} %get-tuple-element.31), channel_id=1, source_target_pairs={{0,8},{4,12},{8,0},{12,4},{1,9},{5,13},{9,1},{13,5},{2,10},{6,14},... | collective-permute-start | bytes 983048 | tf_op jit(solution)/shard_map/ppermute | solution.py:402
  6.0 1.8 %collective-permute-start.10 = (bf16[128,1024]{1,0:T(8,128)(2,1)S(1)}, bf16[128,1024]{1,0:T(8,128)(2,1)S(1)}, u32[]{:S(2)}, u32[]{:S(2)}) collective-permute-start(bf16[128,1024]{1,0:T(8,128)(2,1)S(1)} %get-tuple-element.33), channel_id=1, source_target_pairs={{0,8},{4,12},{8,0},{12,4},{1,9},{5,13},{9,1},{13,5},{2,10},{6,14},... | collective-permute-start | bytes 786440 | tf_op jit(solution)/shard_map/ppermute | solution.py:402
  7.8 6.2 %collective-permute-done.7 = bf16[128,1280]{1,0:T(8,128)(2,1)S(1)} collective-permute-done((bf16[128,1280]{1,0:T(8,128)(2,1)S(1)}, bf16[128,1280]{1,0:T(8,128)(2,1)S(1)}, u32[]{:S(2)}, u32[]{:S(2)}) %collective-permute-start.7) | collective-permute-done | bytes 327712 | tf_op jit(solution)/shard_map/ppermute | solution.py:402
  14.0 5.9 %shard_map.82 = (bf16[1792,2,1024]{2,1,0:T(2,128)(2,1)S(1)}, bf16[1280,2,1024]{2,1,0:T(2,128)(2,1)S(1)}, bf16[1024,2,1024]{2,1,0:T(2,128)(2,1)S(1)}) custom-call(bf16[4096,2,1024]{2,1,0:T(2,128)(2,1)} %src.1), custom_call_target="tpu_custom_call" | custom-call | flops 7000000000 | bytes 16777216 | tf_op jit(solution)/shard_map/pallas_call | solution.py:160
  20.0 3.0 %query_rows.1.refs_0_ = bf16[128,1024]{1,0:T(8,128)(2,1)S(1)} custom-call(bf16[128,4096]{1,0:T(8,128)(2,1)S(1)} %bitcast.19, bf16[32,128]{1,0:T(8,128)(2,1)S(1)} %bitcast.25, bf16[4096,1024]{1,0:T(8,128)(2,1)S(1)} %bitcast.22), custom_call_target="tpu_custom_call" | custom-call | flops 3000000000 | bytes 8388608 | tf_op jit(solution)/shard_map/query_rows/pallas_call | solution.py:89
  23.1 0.6 collective-permute-start.9
  23.9 2.1 %collective-permute-start = (bf16[128,1024]{1,0:T(8,128)(2,1)S(1)}, bf16[128,1024]{1,0:T(8,128)(2,1)S(1)}, u32[]{:S(2)}, u32[]{:S(2)}) collective-permute-start(bf16[128,1024]{1,0:T(8,128)(2,1)S(1)} %query_rows.1.refs_0_), channel_id=1, source_target_pairs={{0,1},{1,2},{2,3},{3,0},{4,5},{5,6},{6,7},{7,4},{8,9},{9,10},{10,1... | collective-permute-start | bytes 786440 | tf_op jit(solution)/shard_map/ppermute | solution.py:411
  26.0 3.0 %fusion.2 = f32[512,2,1024]{2,0,1:T(8,128)S(1)} fusion(bf16[1280,2,1024]{2,1,0:T(2,128)(2,1)S(1)} %get-tuple-element.32, bf16[128,1280]{1,0:T(8,128)(2,1)S(1)} %collective-permute-done.8, bf16[128,1280]{1,0:T(8,128)(2,1)S(1)} %collective-permute-done.7, bf16[128,1280]{1,0:T(8,128)(2,1)S(1)} %collective-permute-done.6, ...), kind=kOutput, calls=%fused_computation.2 | convolution fusion | flops 2689597440 | bytes 10747904 | tf_op jit(solution)/shard_map/rd,dkc->rkc/dot_general | solution.py:422
  29.0 2.7 %collective-permute-start.1 = (bf16[128,1024]{1,0:T(8,128)(2,1)S(1)}, bf16[128,1024]{1,0:T(8,128)(2,1)S(1)}, u32[]{:S(2)}, u32[]{:S(2)}) collective-permute-start(bf16[128,1024]{1,0:T(8,128)(2,1)S(1)} %query_rows.1.refs_0_), channel_id=1, source_target_pairs={{0,2},{1,3},{2,0},{3,1},{4,6},{5,7},{6,4},{7,5},{8,10},{9,11},{10,... | collective-permute-start | bytes 786440 | tf_op jit(solution)/shard_map/ppermute | solution.py:411
  31.6 1.4 %collective-permute-start.2 = (bf16[128,1024]{1,0:T(8,128)(2,1)S(1)}, bf16[128,1024]{1,0:T(8,128)(2,1)S(1)}, u32[]{:S(2)}, u32[]{:S(2)}) collective-permute-start(bf16[128,1024]{1,0:T(8,128)(2,1)S(1)} %query_rows.1.refs_0_), channel_id=1, source_target_pairs={{0,3},{1,0},{2,1},{3,2},{4,7},{5,4},{6,5},{7,6},{8,11},{9,8},{10,9... | collective-permute-start | bytes 786440 | tf_op jit(solution)/shard_map/ppermute | solution.py:411
  33.0 6.0 %fusion = f32[512,2,1024]{2,0,1:T(8,128)} fusion(bf16[1792,2,1024]{2,1,0:T(2,128)(2,1)S(1)} %copy-done.6, bf16[128,1792]{1,0:T(8,128)(2,1)S(1)} %collective-permute-done.5, bf16[128,1792]{1,0:T(8,128)(2,1)S(1)} %collective-permute-done.4, bf16[128,1792]{1,0:T(8,128)(2,1)S(1)} %collective-permute-done.3, bf16[128,1792]{1,0:T(8,128)(2,1)S(1)} %get-tuple-element.29), kind=kOutput, calls=%fused_computation | convolution fusion | flops 3765436416 | bytes 13369344 | tf_op jit(solution)/shard_map/rd,dkc->rkc/dot_general | solution.py:422
  39.0 4.7 %fusion.6.refs_4_ = bf16[2,512,1024]{2,1,0:T(8,128)(2,1)S(1)} fusion(f32[512,2,1024]{2,0,1:T(8,128)} %fusion, f32[512,2,1024]{2,0,1:T(8,128)S(1)} %fusion.2, bf16[1024,2,1024]{2,1,0:T(2,128)(2,1)S(1)} %get-tuple-element.34, bf16[128,1024]{1,0:T(8,128)(2,1)S(1)} %collective-permute-done.11, bf16[128,1024]{1,0:T(8,128)(2,1)S(1)} %collective-permute-done.10, ...), kind=kOutput, calls=%fused_computation.7 | convolution fusion | flops 2154823680 | bytes 15728640 | tf_op jit(solution)/shard_map/rd,dkc->rkc/dot_general | solution.py:422
  43.8 1.9 %collective-permute-done.1.refs_2_ = bf16[128,1024]{1,0:T(8,128)(2,1)S(1)} collective-permute-done((bf16[128,1024]{1,0:T(8,128)(2,1)S(1)}, bf16[128,1024]{1,0:T(8,128)(2,1)S(1)}, u32[]{:S(2)}, u32[]{:S(2)}) %collective-permute-start.1) | collective-permute-done | bytes 262176 | tf_op jit(solution)/shard_map/ppermute | solution.py:411
  45.8 2.9 %attend.1 = (bf16[64,1152]{1,0:T(8,128)(2,1)S(1)}, bf16[64,1024]{1,0:T(8,128)(2,1)S(1)}, bf16[64,1152]{1,0:T(8,128)(2,1)S(1)}, bf16[64,1024]{1,0:T(8,128)(2,1)S(...) custom-call(s32[4,4]{1,0:T(4,128)S(1)} %bitcast.20, ...), custom_call_target="tpu_custom_call" | custom-call | flops 268435456 | bytes 2097152 | tf_op jit(solution)/shard_map/attend/pallas_call | solution.py:308
  48.6 6.1 %collective-permute-start.18 = (bf16[64,1024]{1,0:T(8,128)(2,1)S(1)}, bf16[64,1024]{1,0:T(8,128)(2,1)S(1)}, u32[]{:S(2)}, u32[]{:S(2)}) collective-permute-start(bf16[64,1024]{1,0:T(8,128)(2,1)S(1)} %get-tuple-element.46), channel_id=1, source_target_pairs={{0,1},{1,2},{2,3},{3,0},{4,5},{5,6},{6,7},{7,4},{8,9},{9,10},{10,1... | collective-permute-start | bytes 393224 | tf_op jit(solution)/shard_map/ppermute | solution.py:437
  54.8 1.6 %collective-permute-start.13 = (bf16[64,1152]{1,0:T(8,128)(2,1)S(1)}, bf16[64,1152]{1,0:T(8,128)(2,1)S(1)}, u32[]{:S(2)}, u32[]{:S(2)}) collective-permute-start(bf16[64,1152]{1,0:T(8,128)(2,1)S(1)} %get-tuple-element.38), channel_id=1, source_target_pairs={{0,2},{1,3},{2,0},{3,1},{4,6},{5,7},{6,4},{7,5},{8,10},{9,11},{10,... | collective-permute-start | bytes 442376 | tf_op jit(solution)/shard_map/ppermute | solution.py:437
  56.4 2.9 %collective-permute-start.14 = (bf16[64,1152]{1,0:T(8,128)(2,1)S(1)}, bf16[64,1152]{1,0:T(8,128)(2,1)S(1)}, u32[]{:S(2)}, u32[]{:S(2)}) collective-permute-start(bf16[64,1152]{1,0:T(8,128)(2,1)S(1)} %get-tuple-element.39), channel_id=1, source_target_pairs={{0,3},{1,0},{2,1},{3,2},{4,7},{5,4},{6,5},{7,6},{8,11},{9,8},{10,9... | collective-permute-start | bytes 442376 | tf_op jit(solution)/shard_map/ppermute | solution.py:437
  59.3 1.3 %collective-permute-start.19 = (bf16[64,1024]{1,0:T(8,128)(2,1)S(1)}, bf16[64,1024]{1,0:T(8,128)(2,1)S(1)}, u32[]{:S(2)}, u32[]{:S(2)}) collective-permute-start(bf16[64,1024]{1,0:T(8,128)(2,1)S(1)} %get-tuple-element.47), channel_id=1, source_target_pairs={{0,2},{1,3},{2,0},{3,1},{4,6},{5,7},{6,4},{7,5},{8,10},{9,11},{10,... | collective-permute-start | bytes 393224 | tf_op jit(solution)/shard_map/ppermute | solution.py:437
  60.6 1.3 %collective-permute-start.20 = (bf16[64,1024]{1,0:T(8,128)(2,1)S(1)}, bf16[64,1024]{1,0:T(8,128)(2,1)S(1)}, u32[]{:S(2)}, u32[]{:S(2)}) collective-permute-start(bf16[64,1024]{1,0:T(8,128)(2,1)S(1)} %get-tuple-element.48), channel_id=1, source_target_pairs={{0,3},{1,0},{2,1},{3,2},{4,7},{5,4},{6,5},{7,6},{8,11},{9,8},{10,9... | collective-permute-start | bytes 393224 | tf_op jit(solution)/shard_map/ppermute | solution.py:437
  62.0 3.5 %shard_map.83.refs_8_ = bf16[1024,4096]{1,0:T(8,128)(2,1)S(1)} custom-call(bf16[1024,4096]{1,0:T(8,128)(2,1)} %src.2), custom_call_target="tpu_custom_call" | custom-call | flops 7000000000 | bytes 8388608 | tf_op jit(solution)/shard_map/pallas_call | solution.py:160
  65.5 11.8 %collective-permute-done.19.refs_2_ = bf16[64,1024]{1,0:T(8,128)(2,1)S(1)} collective-permute-done((bf16[64,1024]{1,0:T(8,128)(2,1)S(1)}, bf16[64,1024]{1,0:T(8,128)(2,1)S(1)}, u32[]{:S(2)}, u32[]{:S(2)}) %collective-permute-start.19) | collective-permute-done | bytes 131104 | tf_op jit(solution)/shard_map/ppermute | solution.py:437
  77.3 2.0 %project.3 = (bf16[64,1024]{1,0:T(8,128)(2,1)S(1)}, bf16[64,1024]{1,0:T(8,128)(2,1)S(1)}, bf16[64,1024]{1,0:T(8,128)(2,1)S(1)}, bf16[64,1024]{1,0:T(8,128)(2,1)S(1)}) custom-call(bf16[64,1024]{1,0:T(8,128)(2,1)S(1)} %get-tuple-element.45.refs_0_, bf16[64,1024]{1,0:T(8,128)(2,1)S(1)} %collective-permute-done.18.refs_1_, ...), custom_call_target="tpu_custom_call" | custom-call | flops 536870912 | bytes 8388608 | tf_op jit(solution)/shard_map/project/pallas_call | solution.py:371
  79.4 1.6 %collective-permute-start.22 = (bf16[64,1024]{1,0:T(8,128)(2,1)S(1)}, bf16[64,1024]{1,0:T(8,128)(2,1)S(1)}, u32[]{:S(2)}, u32[]{:S(2)}) collective-permute-start(bf16[64,1024]{1,0:T(8,128)(2,1)S(1)} %get-tuple-element.51), channel_id=1, source_target_pairs={{0,8},{4,12},{8,0},{12,4},{1,9},{5,13},{9,1},{13,5},{2,10},{6,14},... | collective-permute-start | bytes 393224 | tf_op jit(solution)/shard_map/ppermute | solution.py:443
  81.2 2.0 %project.2 = (bf16[64,1024]{1,0:T(8,128)(2,1)S(1)}, bf16[64,1024]{1,0:T(8,128)(2,1)S(1)}, bf16[64,1024]{1,0:T(8,128)(2,1)S(1)}, bf16[64,1024]{1,0:T(8,128)(2,1)S(1)}) custom-call(bf16[64,1152]{1,0:T(8,128)(2,1)S(1)} %get-tuple-element.36.refs_0_.refs_4_, bf16[64,1152]{1,0:T(8,128)(2,1)S(1)} %collective-permute-done.12.refs_1_.refs_5_, ...), custom_call_target="tpu_custom_call" | custom-call | flops 536870912 | bytes 8388608 | tf_op jit(solution)/shard_map/project/pallas_call | solution.py:371
  83.7 1.5 %collective-permute-start.16 = (bf16[64,1024]{1,0:T(8,128)(2,1)S(1)}, bf16[64,1024]{1,0:T(8,128)(2,1)S(1)}, u32[]{:S(2)}, u32[]{:S(2)}) collective-permute-start(bf16[64,1024]{1,0:T(8,128)(2,1)S(1)} %get-tuple-element.43), channel_id=1, source_target_pairs={{0,8},{4,12},{8,0},{12,4},{1,9},{5,13},{9,1},{13,5},{2,10},{6,14},... | collective-permute-start | bytes 393224 | tf_op jit(solution)/shard_map/ppermute | solution.py:443
  85.2 0.6 collective-permute-done.22.refs_6_
  85.8 1.8 %collective-permute-done.23.refs_7_ = bf16[64,1024]{1,0:T(8,128)(2,1)S(1)} collective-permute-done((bf16[64,1024]{1,0:T(8,128)(2,1)S(1)}, bf16[64,1024]{1,0:T(8,128)(2,1)S(1)}, u32[]{:S(2)}, u32[]{:S(2)}) %collective-permute-start.23) | collective-permute-done | bytes 131104 | tf_op jit(solution)/shard_map/ppermute | solution.py:443
  87.6 3.8 %collective-permute-done.16.refs_2_ = bf16[64,1024]{1,0:T(8,128)(2,1)S(1)} collective-permute-done((bf16[64,1024]{1,0:T(8,128)(2,1)S(1)}, bf16[64,1024]{1,0:T(8,128)(2,1)S(1)}, u32[]{:S(2)}, u32[]{:S(2)}) %collective-permute-start.16) | collective-permute-done | bytes 131104 | tf_op jit(solution)/shard_map/ppermute | solution.py:443
  91.4 1.7 %collective-permute-done.17.refs_3_ = bf16[64,1024]{1,0:T(8,128)(2,1)S(1)} collective-permute-done((bf16[64,1024]{1,0:T(8,128)(2,1)S(1)}, bf16[64,1024]{1,0:T(8,128)(2,1)S(1)}, u32[]{:S(2)}, u32[]{:S(2)}) %collective-permute-start.17) | collective-permute-done | bytes 131104 | tf_op jit(solution)/shard_map/ppermute | solution.py:443
  93.1 0.9 sum_parts.1
  (46 shorter events, 2.2 us)
Async XLA Ops:
  0.0 1.2 %copy-start.2 = (bf16[1,1,128,4096]{3,2,1,0:T(8,128)(2,1)S(1)}, bf16[1,1,128,4096]{3,2,1,0:T(8,128)(2,1)}, u32[]{:S(2)}) copy-start(bf16[1,1,128,4096]{3,2,1,0:T(8,128)(2,1)} %param.8) | copy-start | bytes 3145732
  2.4 11.6 %collective-permute-start.7 = (bf16[128,1280]{1,0:T(8,128)(2,1)S(1)}, bf16[128,1280]{1,0:T(8,128)(2,1)S(1)}, u32[]{:S(2)}, u32[]{:S(2)}) collective-permute-start(bf16[128,1280]{1,0:T(8,128)(2,1)S(1)} %get-tuple-element.31), channel_id=1, source_target_pairs={{0,8},{4,12},{8,0},{12,4},{1,9},{5,13},{9,1},{13,5},{2,10},{6,14},... | collective-permute-start | bytes 983048 | tf_op jit(solution)/shard_map/ppermute | solution.py:402
  5.5 17.6 %collective-permute-start.6 = (bf16[128,1280]{1,0:T(8,128)(2,1)S(1)}, bf16[128,1280]{1,0:T(8,128)(2,1)S(1)}, u32[]{:S(2)}, u32[]{:S(2)}) collective-permute-start(bf16[128,1280]{1,0:T(8,128)(2,1)S(1)} %get-tuple-element.31), channel_id=1, source_target_pairs={{0,4},{4,0},{8,12},{12,8},{1,5},{5,1},{9,13},{13,9},{2,6},{6,2},{1... | collective-permute-start | bytes 983048 | tf_op jit(solution)/shard_map/ppermute | solution.py:405
  5.5 18.4 %collective-permute-start.4 = (bf16[128,1792]{1,0:T(8,128)(2,1)S(1)}, bf16[128,1792]{1,0:T(8,128)(2,1)S(1)}, u32[]{:S(2)}, u32[]{:S(2)}) collective-permute-start(bf16[128,1792]{1,0:T(8,128)(2,1)S(1)} %get-tuple-element.29), channel_id=1, source_target_pairs={{0,8},{4,12},{8,0},{12,4},{1,9},{5,13},{9,1},{13,5},{2,10},{6,14},... | collective-permute-start | bytes 1376264 | tf_op jit(solution)/shard_map/ppermute | solution.py:402
  5.6 26.0 %collective-permute-start.3 = (bf16[128,1792]{1,0:T(8,128)(2,1)S(1)}, bf16[128,1792]{1,0:T(8,128)(2,1)S(1)}, u32[]{:S(2)}, u32[]{:S(2)}) collective-permute-start(bf16[128,1792]{1,0:T(8,128)(2,1)S(1)} %get-tuple-element.29), channel_id=1, source_target_pairs={{0,4},{4,0},{8,12},{12,8},{1,5},{5,1},{9,13},{13,9},{2,6},{6,2},{1... | collective-permute-start | bytes 1376264 | tf_op jit(solution)/shard_map/ppermute | solution.py:405
  6.0 14.0 %slice-start = ((s8[8388608]{0:T(1024)(128)(4,1)}), s8[4194304]{0:T(1024)(128)(4,1)S(1)}, s32[]{:S(2)}) async-start(s8[8388608]{0:T(1024)(128)(4,1)} %bitcast.21), calls=%async_computation | async-start | bytes 8388608
  6.0 14.0 %copy-start = (bf16[2,64,4096]{2,1,0:T(8,128)(2,1)S(1)}, bf16[2,64,4096]{2,1,0:T(8,128)(2,1)}, u32[]{:S(2)}) copy-start(bf16[2,64,4096]{2,1,0:T(8,128)(2,1)} %res_ref.1) | copy-start | bytes 3145732
  6.0 14.0 %slice-start.1 = ((s8[8388608]{0:T(1024)(128)(4,1)}), s8[4194304]{0:T(1024)(128)(4,1)S(1)}, s32[]{:S(2)}) async-start(s8[8388608]{0:T(1024)(128)(4,1)} %bitcast.21), calls=%async_computation.1 | async-start | bytes 8388608
  6.0 14.0 %copy-start.4 = (bf16[4096]{0:T(1024)(128)(2,1)S(1)}, bf16[4096]{0:T(1024)(128)(2,1)}, u32[]{:S(2)}) copy-start(bf16[4096]{0:T(1024)(128)(2,1)} %param.11) | copy-start | bytes 24580
  6.0 23.0 %collective-permute-start.10 = (bf16[128,1024]{1,0:T(8,128)(2,1)S(1)}, bf16[128,1024]{1,0:T(8,128)(2,1)S(1)}, u32[]{:S(2)}, u32[]{:S(2)}) collective-permute-start(bf16[128,1024]{1,0:T(8,128)(2,1)S(1)} %get-tuple-element.33), channel_id=1, source_target_pairs={{0,8},{4,12},{8,0},{12,4},{1,9},{5,13},{9,1},{13,5},{2,10},{6,14},... | collective-permute-start | bytes 786440 | tf_op jit(solution)/shard_map/ppermute | solution.py:402
  14.0 11.9 %collective-permute-start.8 = (bf16[128,1280]{1,0:T(8,128)(2,1)S(1)}, bf16[128,1280]{1,0:T(8,128)(2,1)S(1)}, u32[]{:S(2)}, u32[]{:S(2)}) collective-permute-start(bf16[128,1280]{1,0:T(8,128)(2,1)S(1)} %collective-permute-done.7), channel_id=1, source_target_pairs={{0,4},{4,0},{8,12},{12,8},{1,5},{5,1},{9,13},{13,9},{2,6},{6,2},{1... | collective-permute-start | bytes 983048 | tf_op jit(solution)/shard_map/ppermute | solution.py:405
  20.0 3.1 %copy-start.5 = (bf16[1792,2,1024]{2,1,0:T(2,128)(2,1)}, bf16[1792,2,1024]{2,1,0:T(2,128)(2,1)S(1)}, u32[]{:S(2)}) copy-start(bf16[1792,2,1024]{2,1,0:T(2,128)(2,1)S(1)} %get-tuple-element.30) | copy-start | bytes 22020100
  23.1 15.9 %collective-permute-start.9 = (bf16[128,1024]{1,0:T(8,128)(2,1)S(1)}, bf16[128,1024]{1,0:T(8,128)(2,1)S(1)}, u32[]{:S(2)}, u32[]{:S(2)}) collective-permute-start(bf16[128,1024]{1,0:T(8,128)(2,1)S(1)} %get-tuple-element.33), channel_id=1, source_target_pairs={{0,4},{4,0},{8,12},{12,8},{1,5},{5,1},{9,13},{13,9},{2,6},{6,2},{1... | collective-permute-start | bytes 786440 | tf_op jit(solution)/shard_map/ppermute | solution.py:405
  23.9 19.9 %collective-permute-start = (bf16[128,1024]{1,0:T(8,128)(2,1)S(1)}, bf16[128,1024]{1,0:T(8,128)(2,1)S(1)}, u32[]{:S(2)}, u32[]{:S(2)}) collective-permute-start(bf16[128,1024]{1,0:T(8,128)(2,1)S(1)} %query_rows.1.refs_0_), channel_id=1, source_target_pairs={{0,1},{1,2},{2,3},{3,0},{4,5},{5,6},{6,7},{7,4},{8,9},{9,10},{10,1... | collective-permute-start | bytes 786440 | tf_op jit(solution)/shard_map/ppermute | solution.py:411
  26.0 7.0 %collective-permute-start.5 = (bf16[128,1792]{1,0:T(8,128)(2,1)S(1)}, bf16[128,1792]{1,0:T(8,128)(2,1)S(1)}, u32[]{:S(2)}, u32[]{:S(2)}) collective-permute-start(bf16[128,1792]{1,0:T(8,128)(2,1)S(1)} %collective-permute-done.4), channel_id=1, source_target_pairs={{0,4},{4,0},{8,12},{12,8},{1,5},{5,1},{9,13},{13,9},{2,6},{6,2},{1... | collective-permute-start | bytes 1376264 | tf_op jit(solution)/shard_map/ppermute | solution.py:405
  26.0 7.0 %copy-start.6 = (bf16[1792,2,1024]{2,1,0:T(2,128)(2,1)S(1)}, bf16[1792,2,1024]{2,1,0:T(2,128)(2,1)}, u32[]{:S(2)}) copy-start(bf16[1792,2,1024]{2,1,0:T(2,128)(2,1)} %copy-done.5) | copy-start | bytes 22020100
  29.0 16.7 %collective-permute-start.1 = (bf16[128,1024]{1,0:T(8,128)(2,1)S(1)}, bf16[128,1024]{1,0:T(8,128)(2,1)S(1)}, u32[]{:S(2)}, u32[]{:S(2)}) collective-permute-start(bf16[128,1024]{1,0:T(8,128)(2,1)S(1)} %query_rows.1.refs_0_), channel_id=1, source_target_pairs={{0,2},{1,3},{2,0},{3,1},{4,6},{5,7},{6,4},{7,5},{8,10},{9,11},{10,... | collective-permute-start | bytes 786440 | tf_op jit(solution)/shard_map/ppermute | solution.py:411
  31.6 14.1 %collective-permute-start.2 = (bf16[128,1024]{1,0:T(8,128)(2,1)S(1)}, bf16[128,1024]{1,0:T(8,128)(2,1)S(1)}, u32[]{:S(2)}, u32[]{:S(2)}) collective-permute-start(bf16[128,1024]{1,0:T(8,128)(2,1)S(1)} %query_rows.1.refs_0_), channel_id=1, source_target_pairs={{0,3},{1,0},{2,1},{3,2},{4,7},{5,4},{6,5},{7,6},{8,11},{9,8},{10,9... | collective-permute-start | bytes 786440 | tf_op jit(solution)/shard_map/ppermute | solution.py:411
  33.0 6.1 %collective-permute-start.11 = (bf16[128,1024]{1,0:T(8,128)(2,1)S(1)}, bf16[128,1024]{1,0:T(8,128)(2,1)S(1)}, u32[]{:S(2)}, u32[]{:S(2)}) collective-permute-start(bf16[128,1024]{1,0:T(8,128)(2,1)S(1)} %collective-permute-done.10), channel_id=1, source_target_pairs={{0,4},{4,0},{8,12},{12,8},{1,5},{5,1},{9,13},{13,9},{2,6},{6,2},{1... | collective-permute-start | bytes 786440 | tf_op jit(solution)/shard_map/ppermute | solution.py:405
  39.0 6.7 %copy-start.1 = (s32[4,4,1]{1,2,0:T(1,128)S(1)}, s32[4,4,1]{1,2,0:T(1,128)}, u32[]{:S(2)}) copy-start(s32[4,4,1]{1,2,0:T(1,128)} %param.15) | copy-start | bytes 196
  48.6 12.0 %collective-permute-start.18 = (bf16[64,1024]{1,0:T(8,128)(2,1)S(1)}, bf16[64,1024]{1,0:T(8,128)(2,1)S(1)}, u32[]{:S(2)}, u32[]{:S(2)}) collective-permute-start(bf16[64,1024]{1,0:T(8,128)(2,1)S(1)} %get-tuple-element.46), channel_id=1, source_target_pairs={{0,1},{1,2},{2,3},{3,0},{4,5},{5,6},{6,7},{7,4},{8,9},{9,10},{10,1... | collective-permute-start | bytes 393224 | tf_op jit(solution)/shard_map/ppermute | solution.py:437
  54.8 22.5 %collective-permute-start.12 = (bf16[64,1152]{1,0:T(8,128)(2,1)S(1)}, bf16[64,1152]{1,0:T(8,128)(2,1)S(1)}, u32[]{:S(2)}, u32[]{:S(2)}) collective-permute-start(bf16[64,1152]{1,0:T(8,128)(2,1)S(1)} %get-tuple-element.37), channel_id=1, source_target_pairs={{0,1},{1,2},{2,3},{3,0},{4,5},{5,6},{6,7},{7,4},{8,9},{9,10},{10,1... | collective-permute-start | bytes 442376 | tf_op jit(solution)/shard_map/ppermute | solution.py:437
  54.8 22.4 %collective-permute-start.13 = (bf16[64,1152]{1,0:T(8,128)(2,1)S(1)}, bf16[64,1152]{1,0:T(8,128)(2,1)S(1)}, u32[]{:S(2)}, u32[]{:S(2)}) collective-permute-start(bf16[64,1152]{1,0:T(8,128)(2,1)S(1)} %get-tuple-element.38), channel_id=1, source_target_pairs={{0,2},{1,3},{2,0},{3,1},{4,6},{5,7},{6,4},{7,5},{8,10},{9,11},{10,... | collective-permute-start | bytes 442376 | tf_op jit(solution)/shard_map/ppermute | solution.py:437
  56.4 20.8 %collective-permute-start.14 = (bf16[64,1152]{1,0:T(8,128)(2,1)S(1)}, bf16[64,1152]{1,0:T(8,128)(2,1)S(1)}, u32[]{:S(2)}, u32[]{:S(2)}) collective-permute-start(bf16[64,1152]{1,0:T(8,128)(2,1)S(1)} %get-tuple-element.39), channel_id=1, source_target_pairs={{0,3},{1,0},{2,1},{3,2},{4,7},{5,4},{6,5},{7,6},{8,11},{9,8},{10,9... | collective-permute-start | bytes 442376 | tf_op jit(solution)/shard_map/ppermute | solution.py:437
  59.3 17.9 %collective-permute-start.19 = (bf16[64,1024]{1,0:T(8,128)(2,1)S(1)}, bf16[64,1024]{1,0:T(8,128)(2,1)S(1)}, u32[]{:S(2)}, u32[]{:S(2)}) collective-permute-start(bf16[64,1024]{1,0:T(8,128)(2,1)S(1)} %get-tuple-element.47), channel_id=1, source_target_pairs={{0,2},{1,3},{2,0},{3,1},{4,6},{5,7},{6,4},{7,5},{8,10},{9,11},{10,... | collective-permute-start | bytes 393224 | tf_op jit(solution)/shard_map/ppermute | solution.py:437
  60.6 16.6 %collective-permute-start.20 = (bf16[64,1024]{1,0:T(8,128)(2,1)S(1)}, bf16[64,1024]{1,0:T(8,128)(2,1)S(1)}, u32[]{:S(2)}, u32[]{:S(2)}) collective-permute-start(bf16[64,1024]{1,0:T(8,128)(2,1)S(1)} %get-tuple-element.48), channel_id=1, source_target_pairs={{0,3},{1,0},{2,1},{3,2},{4,7},{5,4},{6,5},{7,6},{8,11},{9,8},{10,9... | collective-permute-start | bytes 393224 | tf_op jit(solution)/shard_map/ppermute | solution.py:437
  79.3 5.9 %collective-permute-start.21 = (bf16[64,1024]{1,0:T(8,128)(2,1)S(1)}, bf16[64,1024]{1,0:T(8,128)(2,1)S(1)}, u32[]{:S(2)}, u32[]{:S(2)}) collective-permute-start(bf16[64,1024]{1,0:T(8,128)(2,1)S(1)} %get-tuple-element.50), channel_id=1, source_target_pairs={{0,4},{4,0},{8,12},{12,8},{1,5},{5,1},{9,13},{13,9},{2,6},{6,2},{1... | collective-permute-start | bytes 393224 | tf_op jit(solution)/shard_map/ppermute | solution.py:443
  79.4 6.4 %collective-permute-start.22 = (bf16[64,1024]{1,0:T(8,128)(2,1)S(1)}, bf16[64,1024]{1,0:T(8,128)(2,1)S(1)}, u32[]{:S(2)}, u32[]{:S(2)}) collective-permute-start(bf16[64,1024]{1,0:T(8,128)(2,1)S(1)} %get-tuple-element.51), channel_id=1, source_target_pairs={{0,8},{4,12},{8,0},{12,4},{1,9},{5,13},{9,1},{13,5},{2,10},{6,14},... | collective-permute-start | bytes 393224 | tf_op jit(solution)/shard_map/ppermute | solution.py:443
  80.9 6.7 %collective-permute-start.23 = (bf16[64,1024]{1,0:T(8,128)(2,1)S(1)}, bf16[64,1024]{1,0:T(8,128)(2,1)S(1)}, u32[]{:S(2)}, u32[]{:S(2)}) collective-permute-start(bf16[64,1024]{1,0:T(8,128)(2,1)S(1)} %get-tuple-element.52), channel_id=1, source_target_pairs={{0,12},{4,8},{8,4},{12,0},{1,13},{5,9},{9,5},{13,1},{2,14},{6,10},... | collective-permute-start | bytes 393224 | tf_op jit(solution)/shard_map/ppermute | solution.py:443
  83.2 4.4 %collective-permute-start.15 = (bf16[64,1024]{1,0:T(8,128)(2,1)S(1)}, bf16[64,1024]{1,0:T(8,128)(2,1)S(1)}, u32[]{:S(2)}, u32[]{:S(2)}) collective-permute-start(bf16[64,1024]{1,0:T(8,128)(2,1)S(1)} %get-tuple-element.42), channel_id=1, source_target_pairs={{0,4},{4,0},{8,12},{12,8},{1,5},{5,1},{9,13},{13,9},{2,6},{6,2},{1... | collective-permute-start | bytes 393224 | tf_op jit(solution)/shard_map/ppermute | solution.py:443
  83.7 7.8 %collective-permute-start.16 = (bf16[64,1024]{1,0:T(8,128)(2,1)S(1)}, bf16[64,1024]{1,0:T(8,128)(2,1)S(1)}, u32[]{:S(2)}, u32[]{:S(2)}) collective-permute-start(bf16[64,1024]{1,0:T(8,128)(2,1)S(1)} %get-tuple-element.43), channel_id=1, source_target_pairs={{0,8},{4,12},{8,0},{12,4},{1,9},{5,13},{9,1},{13,5},{2,10},{6,14},... | collective-permute-start | bytes 393224 | tf_op jit(solution)/shard_map/ppermute | solution.py:443
  85.2 8.0 %collective-permute-start.17 = (bf16[64,1024]{1,0:T(8,128)(2,1)S(1)}, bf16[64,1024]{1,0:T(8,128)(2,1)S(1)}, u32[]{:S(2)}, u32[]{:S(2)}) collective-permute-start(bf16[64,1024]{1,0:T(8,128)(2,1)S(1)} %get-tuple-element.44), channel_id=1, source_target_pairs={{0,12},{4,8},{8,4},{12,0},{1,13},{5,9},{9,5},{13,1},{2,14},{6,10},... | collective-permute-start | bytes 393224 | tf_op jit(solution)/shard_map/ppermute | solution.py:443
  (1 other events, 0.7 us)

commit v2 on v1

--- a/solution.py
+++ b/solution.py
@@ -330,7 +330,7 @@
     )(questions, *queries, kv)
 
 
-def project_kernel(heads, parts, number, *refs):
+def project_kernel(heads, parts, number, chips, blocks, *refs):
     part_refs, stat_refs = refs[:parts], refs[parts : 2 * parts]
     w_ref = refs[2 * parts]
     out_refs, rows_ref = refs[2 * parts + 1 : -1], refs[-1]
@@ -352,29 +352,28 @@
     )
     rows_ref[...] = (mixed / functools.reduce(jnp.add, sizes)).astype(BF16)
     piece = out_refs[0].shape[1]
-    chips = len(out_refs) // 2
     me_seq = lax.axis_index("seq")
     chip = lax.div(me_seq, 2)
     core = me_seq - 2 * chip
-    for i, out in enumerate(out_refs):
-        hop, flip = divmod(i, 2)
+    for block, out in zip(blocks, out_refs):
+        hop, flip = divmod(block, 2)
         dest = 2 * lax.rem(chip + hop, chips) + (1 - core if flip else core)
         cut = pl.ds(pl.multiple_of(dest * piece, piece), piece)
         out[...] = jnp.dot(rows_ref[...], w_ref[:, cut], preferred_element_type=F32).astype(BF16)
 
 
-def project(number, partials, stats, weight, count):
+def project(number, partials, stats, weight, count, blocks):
     parts = len(partials)
     rows = partials[0].shape[0]
     cols = weight.shape[0]
     piece = weight.shape[1] // count
     return pl.pallas_call(
-        functools.partial(project_kernel, cols // HD, parts, number),
+        functools.partial(project_kernel, cols // HD, parts, number, count // 2, blocks),
         in_specs=[full_spec()] * (2 * parts + 1),
-        out_specs=[full_spec()] * count,
-        out_shape=[jax.ShapeDtypeStruct((rows, piece), BF16)] * count,
+        out_specs=[full_spec()] * len(blocks),
+        out_shape=[jax.ShapeDtypeStruct((rows, piece), BF16)] * len(blocks),
         scratch_shapes=[pltpu.VMEM((rows, cols), BF16)],
-        cost_estimate=cost(2 * rows * cols * weight.shape[1], cols * weight.shape[1] * 2),
+        cost_estimate=cost(2 * rows * cols * piece * len(blocks), cols * piece * len(blocks) * 2),
         compiler_params=pltpu.CompilerParams(vmem_limit_bytes=16 << 20),
         name="project",
     )(*partials, *stats, weight)
@@ -427,7 +426,7 @@
 
     sent = list(attend(question_of[:, :, 0], all_queries, kv, n_seq, plen, per, dec_len))
     out_source, sent[0] = lax.optimization_barrier((out_weight, sent[0]))
-    (out_part,) = load(out_source, [0, out_weight.shape[0]], 256, 42 << 20)
+    (out_part,) = load(out_source, [0, out_weight.shape[0]], 256, 44 << 20)
     moves = [(hop, f) for hop in range(chips) for f in range(2)]
 
     partials = []
@@ -438,10 +437,12 @@
         )
     parts = []
     for j in range(per):
-        out = project(j, partials[j], partials[0], out_part, n_seq)
-        parts += [out[0]] + [
-            lax.ppermute(out[i], "seq", seq_move(*moves[i])) for i in range(1, len(moves))
-        ]
+        for blocks in (list(range(2, n_seq)), [0, 1]):
+            out = project(j, partials[j], partials[0], out_part, n_seq, blocks)
+            parts += [
+                lax.ppermute(rows, "seq", seq_move(*moves[k])) if k else rows
+                for k, rows in zip(blocks, out)
+            ]
     return sum_parts(me_seq.reshape(1).astype(jnp.int32), dec_states, parts)
 
 

time: 95 us -> 95.6 us (level)
  Pallas kernels: 20.8 us -> 21.9 us
    pallas_call x2 -> x4, Pallas kernels: 4.05 us -> 5.16 us  [project(): pl.pallas_call(functools.partial(project_kernel, cols // HD, parts, numbe...]
  transfers between devices with their start and end apart: 24 -> 24, of which waited for: 9 -> 8; matrix products, arithmetic and copies ran while one was open for 15% -> 14% of each run, Pallas kernels for 15% -> 17%
where the time goes in v2:
time: 95.6 us; the launch traced here: 94.7 us
  starting transfers between devices  29.3 us (31%)
  waiting for transfers between devices  27.6 us (29%)
  Pallas kernels  21.9 us (23%)
  matrix products  13.7 us (14%)
  local copies, waits for them, and re-layouts  1.95 us (2%)
    dot_general x3, matrix products, body(): jnp.einsum('rd,dkc->rkc', jnp.concatenate(chunks, axis=0), weight, prefer...  13.7 us
    ppermute x6, starting transfers between devices, body(): lax.ppermute(sent[hop * per + j], 'qset', set_move(hop))  13.3 us
    ppermute x6, waiting for transfers between devices, body(): lax.ppermute(sent[hop * per + j], 'qset', set_move(hop))  11.8 us
    pallas_call x2, Pallas kernels, load(): pl.pallas_call(functools.partial(load_kernel, cuts, step), in_specs=[pl.B...  9.43 us
    ppermute x6, waiting for transfers between devices, body(): lax.ppermute(rows, 'seq', seq_move(*moves[k]))  7.43 us
    ppermute x3, waiting for transfers between devices, cross(): lax.ppermute(own, 'seq', seq_move(hop, 0))  6.43 us
    ppermute x3, starting transfers between devices, body(): lax.ppermute(queries, 'qset', set_move(hop))  6.11 us
    pallas_call x4, Pallas kernels, project(): pl.pallas_call(functools.partial(project_kernel, cols // HD, parts, numbe...  5.16 us
  transfers between devices with their start and end apart: 24, of which 8 were waited for; matrix products, arithmetic and copies ran while one was open for 14% of the time, Pallas kernels for 17%

profile of v2, /device:TPU:0, one launch (start us, length us, event | category | flops | bytes accessed | tf_op | source)
XLA Modules:
  0.0 94.7 jit_solution(7985701525645787094)
XLA Ops:
  0.0 1.2 %copy-done.2 = bf16[1,1,128,4096]{3,2,1,0:T(8,128)(2,1)S(1)} copy-done((bf16[1,1,128,4096]{3,2,1,0:T(8,128)(2,1)S(1)}, bf16[1,1,128,4096]{3,2,1,0:T(8,128)(2,1)}, u32[]{:S(2)}) %copy-start.2) | copy-done | bytes 1048600
  1.2 0.7 copy-done.3
  2.4 3.0 %collective-permute-start.7 = (bf16[128,1280]{1,0:T(8,128)(2,1)S(1)}, bf16[128,1280]{1,0:T(8,128)(2,1)S(1)}, u32[]{:S(2)}, u32[]{:S(2)}) collective-permute-start(bf16[128,1280]{1,0:T(8,128)(2,1)S(1)} %get-tuple-element.31), channel_id=1, source_target_pairs={{0,8},{4,12},{8,0},{12,4},{1,9},{5,13},{9,1},{13,5},{2,10},{6,14},... | collective-permute-start | bytes 983048 | tf_op jit(solution)/shard_map/ppermute | solution.py:401
  6.0 1.8 %collective-permute-start.10 = (bf16[128,1024]{1,0:T(8,128)(2,1)S(1)}, bf16[128,1024]{1,0:T(8,128)(2,1)S(1)}, u32[]{:S(2)}, u32[]{:S(2)}) collective-permute-start(bf16[128,1024]{1,0:T(8,128)(2,1)S(1)} %get-tuple-element.33), channel_id=1, source_target_pairs={{0,8},{4,12},{8,0},{12,4},{1,9},{5,13},{9,1},{13,5},{2,10},{6,14},... | collective-permute-start | bytes 786440 | tf_op jit(solution)/shard_map/ppermute | solution.py:401
  7.8 6.2 %collective-permute-done.7 = bf16[128,1280]{1,0:T(8,128)(2,1)S(1)} collective-permute-done((bf16[128,1280]{1,0:T(8,128)(2,1)S(1)}, bf16[128,1280]{1,0:T(8,128)(2,1)S(1)}, u32[]{:S(2)}, u32[]{:S(2)}) %collective-permute-start.7) | collective-permute-done | bytes 327712 | tf_op jit(solution)/shard_map/ppermute | solution.py:401
  14.0 5.9 %shard_map.82 = (bf16[1792,2,1024]{2,1,0:T(2,128)(2,1)S(1)}, bf16[1280,2,1024]{2,1,0:T(2,128)(2,1)S(1)}, bf16[1024,2,1024]{2,1,0:T(2,128)(2,1)S(1)}) custom-call(bf16[4096,2,1024]{2,1,0:T(2,128)(2,1)} %src.1), custom_call_target="tpu_custom_call" | custom-call | flops 7000000000 | bytes 16777216 | tf_op jit(solution)/shard_map/pallas_call | solution.py:160
  20.0 3.0 %query_rows.1.refs_0_ = bf16[128,1024]{1,0:T(8,128)(2,1)S(1)} custom-call(bf16[128,4096]{1,0:T(8,128)(2,1)S(1)} %bitcast.19, bf16[32,128]{1,0:T(8,128)(2,1)S(1)} %bitcast.25, bf16[4096,1024]{1,0:T(8,128)(2,1)S(1)} %bitcast.22), custom_call_target="tpu_custom_call" | custom-call | flops 3000000000 | bytes 8388608 | tf_op jit(solution)/shard_map/query_rows/pallas_call | solution.py:89
  23.9 2.1 %collective-permute-start = (bf16[128,1024]{1,0:T(8,128)(2,1)S(1)}, bf16[128,1024]{1,0:T(8,128)(2,1)S(1)}, u32[]{:S(2)}, u32[]{:S(2)}) collective-permute-start(bf16[128,1024]{1,0:T(8,128)(2,1)S(1)} %query_rows.1.refs_0_), channel_id=1, source_target_pairs={{0,1},{1,2},{2,3},{3,0},{4,5},{5,6},{6,7},{7,4},{8,9},{9,10},{10,1... | collective-permute-start | bytes 786440 | tf_op jit(solution)/shard_map/ppermute | solution.py:410
  26.0 3.0 %fusion.2 = f32[512,2,1024]{2,0,1:T(8,128)S(1)} fusion(bf16[1280,2,1024]{2,1,0:T(2,128)(2,1)S(1)} %get-tuple-element.32, bf16[128,1280]{1,0:T(8,128)(2,1)S(1)} %collective-permute-done.8, bf16[128,1280]{1,0:T(8,128)(2,1)S(1)} %collective-permute-done.7, bf16[128,1280]{1,0:T(8,128)(2,1)S(1)} %collective-permute-done.6, ...), kind=kOutput, calls=%fused_computation.2 | convolution fusion | flops 2689597440 | bytes 10747904 | tf_op jit(solution)/shard_map/rd,dkc->rkc/dot_general | solution.py:421
  29.0 2.7 %collective-permute-start.1 = (bf16[128,1024]{1,0:T(8,128)(2,1)S(1)}, bf16[128,1024]{1,0:T(8,128)(2,1)S(1)}, u32[]{:S(2)}, u32[]{:S(2)}) collective-permute-start(bf16[128,1024]{1,0:T(8,128)(2,1)S(1)} %query_rows.1.refs_0_), channel_id=1, source_target_pairs={{0,2},{1,3},{2,0},{3,1},{4,6},{5,7},{6,4},{7,5},{8,10},{9,11},{10,... | collective-permute-start | bytes 786440 | tf_op jit(solution)/shard_map/ppermute | solution.py:410
  31.6 1.3 %collective-permute-start.2 = (bf16[128,1024]{1,0:T(8,128)(2,1)S(1)}, bf16[128,1024]{1,0:T(8,128)(2,1)S(1)}, u32[]{:S(2)}, u32[]{:S(2)}) collective-permute-start(bf16[128,1024]{1,0:T(8,128)(2,1)S(1)} %query_rows.1.refs_0_), channel_id=1, source_target_pairs={{0,3},{1,0},{2,1},{3,2},{4,7},{5,4},{6,5},{7,6},{8,11},{9,8},{10,9... | collective-permute-start | bytes 786440 | tf_op jit(solution)/shard_map/ppermute | solution.py:410
  33.0 6.0 %fusion = f32[512,2,1024]{2,0,1:T(8,128)} fusion(bf16[1792,2,1024]{2,1,0:T(2,128)(2,1)S(1)} %copy-done.6, bf16[128,1792]{1,0:T(8,128)(2,1)S(1)} %collective-permute-done.5, bf16[128,1792]{1,0:T(8,128)(2,1)S(1)} %collective-permute-done.4, bf16[128,1792]{1,0:T(8,128)(2,1)S(1)} %collective-permute-done.3, bf16[128,1792]{1,0:T(8,128)(2,1)S(1)} %get-tuple-element.29), kind=kOutput, calls=%fused_computation | convolution fusion | flops 3765436416 | bytes 13369344 | tf_op jit(solution)/shard_map/rd,dkc->rkc/dot_general | solution.py:421
  39.0 4.7 %fusion.6.refs_4_ = bf16[2,512,1024]{2,1,0:T(8,128)(2,1)S(1)} fusion(f32[512,2,1024]{2,0,1:T(8,128)} %fusion, f32[512,2,1024]{2,0,1:T(8,128)S(1)} %fusion.2, bf16[1024,2,1024]{2,1,0:T(2,128)(2,1)S(1)} %get-tuple-element.34, bf16[128,1024]{1,0:T(8,128)(2,1)S(1)} %collective-permute-done.11, bf16[128,1024]{1,0:T(8,128)(2,1)S(1)} %collective-permute-done.10, ...), kind=kOutput, calls=%fused_computation.7 | convolution fusion | flops 2154823680 | bytes 15728640 | tf_op jit(solution)/shard_map/rd,dkc->rkc/dot_general | solution.py:421
  43.8 1.9 %collective-permute-done.1.refs_2_ = bf16[128,1024]{1,0:T(8,128)(2,1)S(1)} collective-permute-done((bf16[128,1024]{1,0:T(8,128)(2,1)S(1)}, bf16[128,1024]{1,0:T(8,128)(2,1)S(1)}, u32[]{:S(2)}, u32[]{:S(2)}) %collective-permute-start.1) | collective-permute-done | bytes 262176 | tf_op jit(solution)/shard_map/ppermute | solution.py:410
  45.7 2.9 %attend.1 = (bf16[64,1152]{1,0:T(8,128)(2,1)S(1)}, bf16[64,1024]{1,0:T(8,128)(2,1)S(1)}, bf16[64,1152]{1,0:T(8,128)(2,1)S(1)}, bf16[64,1024]{1,0:T(8,128)(2,1)S(...) custom-call(s32[4,4]{1,0:T(4,128)S(1)} %bitcast.20, ...), custom_call_target="tpu_custom_call" | custom-call | flops 268435456 | bytes 2097152 | tf_op jit(solution)/shard_map/attend/pallas_call | solution.py:308
  48.6 6.1 %collective-permute-start.18 = (bf16[64,1024]{1,0:T(8,128)(2,1)S(1)}, bf16[64,1024]{1,0:T(8,128)(2,1)S(1)}, u32[]{:S(2)}, u32[]{:S(2)}) collective-permute-start(bf16[64,1024]{1,0:T(8,128)(2,1)S(1)} %get-tuple-element.46), channel_id=1, source_target_pairs={{0,1},{1,2},{2,3},{3,0},{4,5},{5,6},{6,7},{7,4},{8,9},{9,10},{10,1... | collective-permute-start | bytes 393224 | tf_op jit(solution)/shard_map/ppermute | solution.py:436
  54.8 1.6 %collective-permute-start.13 = (bf16[64,1152]{1,0:T(8,128)(2,1)S(1)}, bf16[64,1152]{1,0:T(8,128)(2,1)S(1)}, u32[]{:S(2)}, u32[]{:S(2)}) collective-permute-start(bf16[64,1152]{1,0:T(8,128)(2,1)S(1)} %get-tuple-element.38), channel_id=1, source_target_pairs={{0,2},{1,3},{2,0},{3,1},{4,6},{5,7},{6,4},{7,5},{8,10},{9,11},{10,... | collective-permute-start | bytes 442376 | tf_op jit(solution)/shard_map/ppermute | solution.py:436
  56.4 2.9 %collective-permute-start.14 = (bf16[64,1152]{1,0:T(8,128)(2,1)S(1)}, bf16[64,1152]{1,0:T(8,128)(2,1)S(1)}, u32[]{:S(2)}, u32[]{:S(2)}) collective-permute-start(bf16[64,1152]{1,0:T(8,128)(2,1)S(1)} %get-tuple-element.39), channel_id=1, source_target_pairs={{0,3},{1,0},{2,1},{3,2},{4,7},{5,4},{6,5},{7,6},{8,11},{9,8},{10,9... | collective-permute-start | bytes 442376 | tf_op jit(solution)/shard_map/ppermute | solution.py:436
  59.3 1.3 %collective-permute-start.19 = (bf16[64,1024]{1,0:T(8,128)(2,1)S(1)}, bf16[64,1024]{1,0:T(8,128)(2,1)S(1)}, u32[]{:S(2)}, u32[]{:S(2)}) collective-permute-start(bf16[64,1024]{1,0:T(8,128)(2,1)S(1)} %get-tuple-element.47), channel_id=1, source_target_pairs={{0,2},{1,3},{2,0},{3,1},{4,6},{5,7},{6,4},{7,5},{8,10},{9,11},{10,... | collective-permute-start | bytes 393224 | tf_op jit(solution)/shard_map/ppermute | solution.py:436
  60.6 1.3 %collective-permute-start.20 = (bf16[64,1024]{1,0:T(8,128)(2,1)S(1)}, bf16[64,1024]{1,0:T(8,128)(2,1)S(1)}, u32[]{:S(2)}, u32[]{:S(2)}) collective-permute-start(bf16[64,1024]{1,0:T(8,128)(2,1)S(1)} %get-tuple-element.48), channel_id=1, source_target_pairs={{0,3},{1,0},{2,1},{3,2},{4,7},{5,4},{6,5},{7,6},{8,11},{9,8},{10,9... | collective-permute-start | bytes 393224 | tf_op jit(solution)/shard_map/ppermute | solution.py:436
  62.0 3.5 %shard_map.83.refs_8_ = bf16[1024,4096]{1,0:T(8,128)(2,1)S(1)} custom-call(bf16[1024,4096]{1,0:T(8,128)(2,1)} %src.2), custom_call_target="tpu_custom_call" | custom-call | flops 7000000000 | bytes 8388608 | tf_op jit(solution)/shard_map/pallas_call | solution.py:160
  65.5 11.8 %collective-permute-done.19.refs_2_ = bf16[64,1024]{1,0:T(8,128)(2,1)S(1)} collective-permute-done((bf16[64,1024]{1,0:T(8,128)(2,1)S(1)}, bf16[64,1024]{1,0:T(8,128)(2,1)S(1)}, u32[]{:S(2)}, u32[]{:S(2)}) %collective-permute-start.19) | collective-permute-done | bytes 131104 | tf_op jit(solution)/shard_map/ppermute | solution.py:436
  77.3 1.3 %project.7 = (bf16[64,1024]{1,0:T(8,128)(2,1)S(1)}, bf16[64,1024]{1,0:T(8,128)(2,1)S(1)}) custom-call(bf16[64,1024]{1,0:T(8,128)(2,1)S(1)} %get-tuple-element.45.refs_0_, bf16[64,1024]{1,0:T(8,128)(2,1)S(1)} %collective-permute-done.18.refs_1_, bf16[64,1024]{1,0:T(8,128)(2,1)S(1)} %collective-permute-done.19.refs_2_, ...), custom_call_target="tpu_custom_call" | custom-call | flops 268435456 | bytes 4194304 | tf_op jit(solution)/shard_map/project/pallas_call | solution.py:370
  78.6 1.3 %project.6 = (bf16[64,1024]{1,0:T(8,128)(2,1)S(1)}, bf16[64,1024]{1,0:T(8,128)(2,1)S(1)}) custom-call(bf16[64,1024]{1,0:T(8,128)(2,1)S(1)} %get-tuple-element.45.refs_0_, bf16[64,1024]{1,0:T(8,128)(2,1)S(1)} %collective-permute-done.18.refs_1_, bf16[64,1024]{1,0:T(8,128)(2,1)S(1)} %collective-permute-done.19.refs_2_, ...), custom_call_target="tpu_custom_call" | custom-call | flops 268435456 | bytes 4194304 | tf_op jit(solution)/shard_map/project/pallas_call | solution.py:370
  79.9 1.6 %collective-permute-start.21 = (bf16[64,1024]{1,0:T(8,128)(2,1)S(1)}, bf16[64,1024]{1,0:T(8,128)(2,1)S(1)}, u32[]{:S(2)}, u32[]{:S(2)}) collective-permute-start(bf16[64,1024]{1,0:T(8,128)(2,1)S(1)} %get-tuple-element.49), channel_id=1, source_target_pairs={{0,8},{4,12},{8,0},{12,4},{1,9},{5,13},{9,1},{13,5},{2,10},{6,14},... | collective-permute-start | bytes 393224 | tf_op jit(solution)/shard_map/ppermute | solution.py:443
  81.9 1.3 %project.5 = (bf16[64,1024]{1,0:T(8,128)(2,1)S(1)}, bf16[64,1024]{1,0:T(8,128)(2,1)S(1)}) custom-call(bf16[64,1152]{1,0:T(8,128)(2,1)S(1)} %get-tuple-element.36.refs_0_.refs_4_, bf16[64,1152]{1,0:T(8,128)(2,1)S(1)} %collective-permute-done.12.refs_1_.refs_5_, bf16[64,1152]{1,0:T(8,128)(2,1)S(1)} %collective-permute-done.13.refs_2_.refs_6_, ...), custom_call_target="tpu_custom_call" | custom-call | flops 268435456 | bytes 4194304 | tf_op jit(solution)/shard_map/project/pallas_call | solution.py:370
  83.5 1.3 %project.4 = (bf16[64,1024]{1,0:T(8,128)(2,1)S(1)}, bf16[64,1024]{1,0:T(8,128)(2,1)S(1)}) custom-call(bf16[64,1152]{1,0:T(8,128)(2,1)S(1)} %get-tuple-element.36.refs_0_.refs_4_, bf16[64,1152]{1,0:T(8,128)(2,1)S(1)} %collective-permute-done.12.refs_1_.refs_5_, bf16[64,1152]{1,0:T(8,128)(2,1)S(1)} %collective-permute-done.13.refs_2_.refs_6_, ...), custom_call_target="tpu_custom_call" | custom-call | flops 268435456 | bytes 4194304 | tf_op jit(solution)/shard_map/project/pallas_call | solution.py:370
  84.8 1.6 %collective-permute-start.15 = (bf16[64,1024]{1,0:T(8,128)(2,1)S(1)}, bf16[64,1024]{1,0:T(8,128)(2,1)S(1)}, u32[]{:S(2)}, u32[]{:S(2)}) collective-permute-start(bf16[64,1024]{1,0:T(8,128)(2,1)S(1)} %get-tuple-element.41), channel_id=1, source_target_pairs={{0,8},{4,12},{8,0},{12,4},{1,9},{5,13},{9,1},{13,5},{2,10},{6,14},... | collective-permute-start | bytes 393224 | tf_op jit(solution)/shard_map/ppermute | solution.py:443
  86.4 1.8 %collective-permute-done.22.refs_5_ = bf16[64,1024]{1,0:T(8,128)(2,1)S(1)} collective-permute-done((bf16[64,1024]{1,0:T(8,128)(2,1)S(1)}, bf16[64,1024]{1,0:T(8,128)(2,1)S(1)}, u32[]{:S(2)}, u32[]{:S(2)}) %collective-permute-start.22) | collective-permute-done | bytes 131104 | tf_op jit(solution)/shard_map/ppermute | solution.py:443
  88.2 3.8 %collective-permute-done.15.refs_0_ = bf16[64,1024]{1,0:T(8,128)(2,1)S(1)} collective-permute-done((bf16[64,1024]{1,0:T(8,128)(2,1)S(1)}, bf16[64,1024]{1,0:T(8,128)(2,1)S(1)}, u32[]{:S(2)}, u32[]{:S(2)}) %collective-permute-start.15) | collective-permute-done | bytes 131104 | tf_op jit(solution)/shard_map/ppermute | solution.py:443
  92.0 1.9 %collective-permute-done.16.refs_1_ = bf16[64,1024]{1,0:T(8,128)(2,1)S(1)} collective-permute-done((bf16[64,1024]{1,0:T(8,128)(2,1)S(1)}, bf16[64,1024]{1,0:T(8,128)(2,1)S(1)}, u32[]{:S(2)}, u32[]{:S(2)}) %collective-permute-start.16) | collective-permute-done | bytes 131104 | tf_op jit(solution)/shard_map/ppermute | solution.py:443
  93.9 0.9 sum_parts.1
  (48 shorter events, 2.8 us)
Async XLA Ops:
  0.0 1.2 %copy-start.2 = (bf16[1,1,128,4096]{3,2,1,0:T(8,128)(2,1)S(1)}, bf16[1,1,128,4096]{3,2,1,0:T(8,128)(2,1)}, u32[]{:S(2)}) copy-start(bf16[1,1,128,4096]{3,2,1,0:T(8,128)(2,1)} %param.8) | copy-start | bytes 3145732
  2.4 11.6 %collective-permute-start.7 = (bf16[128,1280]{1,0:T(8,128)(2,1)S(1)}, bf16[128,1280]{1,0:T(8,128)(2,1)S(1)}, u32[]{:S(2)}, u32[]{:S(2)}) collective-permute-start(bf16[128,1280]{1,0:T(8,128)(2,1)S(1)} %get-tuple-element.31), channel_id=1, source_target_pairs={{0,8},{4,12},{8,0},{12,4},{1,9},{5,13},{9,1},{13,5},{2,10},{6,14},... | collective-permute-start | bytes 983048 | tf_op jit(solution)/shard_map/ppermute | solution.py:401
  5.5 17.6 %collective-permute-start.6 = (bf16[128,1280]{1,0:T(8,128)(2,1)S(1)}, bf16[128,1280]{1,0:T(8,128)(2,1)S(1)}, u32[]{:S(2)}, u32[]{:S(2)}) collective-permute-start(bf16[128,1280]{1,0:T(8,128)(2,1)S(1)} %get-tuple-element.31), channel_id=1, source_target_pairs={{0,4},{4,0},{8,12},{12,8},{1,5},{5,1},{9,13},{13,9},{2,6},{6,2},{1... | collective-permute-start | bytes 983048 | tf_op jit(solution)/shard_map/ppermute | solution.py:404
  5.5 18.4 %collective-permute-start.4 = (bf16[128,1792]{1,0:T(8,128)(2,1)S(1)}, bf16[128,1792]{1,0:T(8,128)(2,1)S(1)}, u32[]{:S(2)}, u32[]{:S(2)}) collective-permute-start(bf16[128,1792]{1,0:T(8,128)(2,1)S(1)} %get-tuple-element.29), channel_id=1, source_target_pairs={{0,8},{4,12},{8,0},{12,4},{1,9},{5,13},{9,1},{13,5},{2,10},{6,14},... | collective-permute-start | bytes 1376264 | tf_op jit(solution)/shard_map/ppermute | solution.py:401
  5.6 26.0 %collective-permute-start.3 = (bf16[128,1792]{1,0:T(8,128)(2,1)S(1)}, bf16[128,1792]{1,0:T(8,128)(2,1)S(1)}, u32[]{:S(2)}, u32[]{:S(2)}) collective-permute-start(bf16[128,1792]{1,0:T(8,128)(2,1)S(1)} %get-tuple-element.29), channel_id=1, source_target_pairs={{0,4},{4,0},{8,12},{12,8},{1,5},{5,1},{9,13},{13,9},{2,6},{6,2},{1... | collective-permute-start | bytes 1376264 | tf_op jit(solution)/shard_map/ppermute | solution.py:404
  6.0 14.0 %slice-start = ((s8[8388608]{0:T(1024)(128)(4,1)}), s8[4194304]{0:T(1024)(128)(4,1)S(1)}, s32[]{:S(2)}) async-start(s8[8388608]{0:T(1024)(128)(4,1)} %bitcast.21), calls=%async_computation | async-start | bytes 8388608
  6.0 14.0 %copy-start = (bf16[2,64,4096]{2,1,0:T(8,128)(2,1)S(1)}, bf16[2,64,4096]{2,1,0:T(8,128)(2,1)}, u32[]{:S(2)}) copy-start(bf16[2,64,4096]{2,1,0:T(8,128)(2,1)} %res_ref.1) | copy-start | bytes 3145732
  6.0 14.0 %slice-start.1 = ((s8[8388608]{0:T(1024)(128)(4,1)}), s8[4194304]{0:T(1024)(128)(4,1)S(1)}, s32[]{:S(2)}) async-start(s8[8388608]{0:T(1024)(128)(4,1)} %bitcast.21), calls=%async_computation.1 | async-start | bytes 8388608
  6.0 14.0 %copy-start.4 = (bf16[4096]{0:T(1024)(128)(2,1)S(1)}, bf16[4096]{0:T(1024)(128)(2,1)}, u32[]{:S(2)}) copy-start(bf16[4096]{0:T(1024)(128)(2,1)} %param.11) | copy-start | bytes 24580
  6.0 23.0 %collective-permute-start.10 = (bf16[128,1024]{1,0:T(8,128)(2,1)S(1)}, bf16[128,1024]{1,0:T(8,128)(2,1)S(1)}, u32[]{:S(2)}, u32[]{:S(2)}) collective-permute-start(bf16[128,1024]{1,0:T(8,128)(2,1)S(1)} %get-tuple-element.33), channel_id=1, source_target_pairs={{0,8},{4,12},{8,0},{12,4},{1,9},{5,13},{9,1},{13,5},{2,10},{6,14},... | collective-permute-start | bytes 786440 | tf_op jit(solution)/shard_map/ppermute | solution.py:401
  14.0 11.9 %collective-permute-start.8 = (bf16[128,1280]{1,0:T(8,128)(2,1)S(1)}, bf16[128,1280]{1,0:T(8,128)(2,1)S(1)}, u32[]{:S(2)}, u32[]{:S(2)}) collective-permute-start(bf16[128,1280]{1,0:T(8,128)(2,1)S(1)} %collective-permute-done.7), channel_id=1, source_target_pairs={{0,4},{4,0},{8,12},{12,8},{1,5},{5,1},{9,13},{13,9},{2,6},{6,2},{1... | collective-permute-start | bytes 983048 | tf_op jit(solution)/shard_map/ppermute | solution.py:404
  20.0 3.1 %copy-start.5 = (bf16[1792,2,1024]{2,1,0:T(2,128)(2,1)}, bf16[1792,2,1024]{2,1,0:T(2,128)(2,1)S(1)}, u32[]{:S(2)}) copy-start(bf16[1792,2,1024]{2,1,0:T(2,128)(2,1)S(1)} %get-tuple-element.30) | copy-start | bytes 22020100
  23.1 15.9 %collective-permute-start.9 = (bf16[128,1024]{1,0:T(8,128)(2,1)S(1)}, bf16[128,1024]{1,0:T(8,128)(2,1)S(1)}, u32[]{:S(2)}, u32[]{:S(2)}) collective-permute-start(bf16[128,1024]{1,0:T(8,128)(2,1)S(1)} %get-tuple-element.33), channel_id=1, source_target_pairs={{0,4},{4,0},{8,12},{12,8},{1,5},{5,1},{9,13},{13,9},{2,6},{6,2},{1... | collective-permute-start | bytes 786440 | tf_op jit(solution)/shard_map/ppermute | solution.py:404
  23.9 19.9 %collective-permute-start = (bf16[128,1024]{1,0:T(8,128)(2,1)S(1)}, bf16[128,1024]{1,0:T(8,128)(2,1)S(1)}, u32[]{:S(2)}, u32[]{:S(2)}) collective-permute-start(bf16[128,1024]{1,0:T(8,128)(2,1)S(1)} %query_rows.1.refs_0_), channel_id=1, source_target_pairs={{0,1},{1,2},{2,3},{3,0},{4,5},{5,6},{6,7},{7,4},{8,9},{9,10},{10,1... | collective-permute-start | bytes 786440 | tf_op jit(solution)/shard_map/ppermute | solution.py:410
  26.0 7.0 %collective-permute-start.5 = (bf16[128,1792]{1,0:T(8,128)(2,1)S(1)}, bf16[128,1792]{1,0:T(8,128)(2,1)S(1)}, u32[]{:S(2)}, u32[]{:S(2)}) collective-permute-start(bf16[128,1792]{1,0:T(8,128)(2,1)S(1)} %collective-permute-done.4), channel_id=1, source_target_pairs={{0,4},{4,0},{8,12},{12,8},{1,5},{5,1},{9,13},{13,9},{2,6},{6,2},{1... | collective-permute-start | bytes 1376264 | tf_op jit(solution)/shard_map/ppermute | solution.py:404
  26.0 7.0 %copy-start.6 = (bf16[1792,2,1024]{2,1,0:T(2,128)(2,1)S(1)}, bf16[1792,2,1024]{2,1,0:T(2,128)(2,1)}, u32[]{:S(2)}) copy-start(bf16[1792,2,1024]{2,1,0:T(2,128)(2,1)} %copy-done.5) | copy-start | bytes 22020100
  29.0 16.7 %collective-permute-start.1 = (bf16[128,1024]{1,0:T(8,128)(2,1)S(1)}, bf16[128,1024]{1,0:T(8,128)(2,1)S(1)}, u32[]{:S(2)}, u32[]{:S(2)}) collective-permute-start(bf16[128,1024]{1,0:T(8,128)(2,1)S(1)} %query_rows.1.refs_0_), channel_id=1, source_target_pairs={{0,2},{1,3},{2,0},{3,1},{4,6},{5,7},{6,4},{7,5},{8,10},{9,11},{10,... | collective-permute-start | bytes 786440 | tf_op jit(solution)/shard_map/ppermute | solution.py:410
  31.6 14.1 %collective-permute-start.2 = (bf16[128,1024]{1,0:T(8,128)(2,1)S(1)}, bf16[128,1024]{1,0:T(8,128)(2,1)S(1)}, u32[]{:S(2)}, u32[]{:S(2)}) collective-permute-start(bf16[128,1024]{1,0:T(8,128)(2,1)S(1)} %query_rows.1.refs_0_), channel_id=1, source_target_pairs={{0,3},{1,0},{2,1},{3,2},{4,7},{5,4},{6,5},{7,6},{8,11},{9,8},{10,9... | collective-permute-start | bytes 786440 | tf_op jit(solution)/shard_map/ppermute | solution.py:410
  33.0 6.0 %collective-permute-start.11 = (bf16[128,1024]{1,0:T(8,128)(2,1)S(1)}, bf16[128,1024]{1,0:T(8,128)(2,1)S(1)}, u32[]{:S(2)}, u32[]{:S(2)}) collective-permute-start(bf16[128,1024]{1,0:T(8,128)(2,1)S(1)} %collective-permute-done.10), channel_id=1, source_target_pairs={{0,4},{4,0},{8,12},{12,8},{1,5},{5,1},{9,13},{13,9},{2,6},{6,2},{1... | collective-permute-start | bytes 786440 | tf_op jit(solution)/shard_map/ppermute | solution.py:404
  39.0 6.7 %copy-start.1 = (s32[4,4,1]{1,2,0:T(1,128)S(1)}, s32[4,4,1]{1,2,0:T(1,128)}, u32[]{:S(2)}) copy-start(s32[4,4,1]{1,2,0:T(1,128)} %param.15) | copy-start | bytes 196
  48.6 12.0 %collective-permute-start.18 = (bf16[64,1024]{1,0:T(8,128)(2,1)S(1)}, bf16[64,1024]{1,0:T(8,128)(2,1)S(1)}, u32[]{:S(2)}, u32[]{:S(2)}) collective-permute-start(bf16[64,1024]{1,0:T(8,128)(2,1)S(1)} %get-tuple-element.46), channel_id=1, source_target_pairs={{0,1},{1,2},{2,3},{3,0},{4,5},{5,6},{6,7},{7,4},{8,9},{9,10},{10,1... | collective-permute-start | bytes 393224 | tf_op jit(solution)/shard_map/ppermute | solution.py:436
  54.8 22.5 %collective-permute-start.12 = (bf16[64,1152]{1,0:T(8,128)(2,1)S(1)}, bf16[64,1152]{1,0:T(8,128)(2,1)S(1)}, u32[]{:S(2)}, u32[]{:S(2)}) collective-permute-start(bf16[64,1152]{1,0:T(8,128)(2,1)S(1)} %get-tuple-element.37), channel_id=1, source_target_pairs={{0,1},{1,2},{2,3},{3,0},{4,5},{5,6},{6,7},{7,4},{8,9},{9,10},{10,1... | collective-permute-start | bytes 442376 | tf_op jit(solution)/shard_map/ppermute | solution.py:436
  54.8 22.4 %collective-permute-start.13 = (bf16[64,1152]{1,0:T(8,128)(2,1)S(1)}, bf16[64,1152]{1,0:T(8,128)(2,1)S(1)}, u32[]{:S(2)}, u32[]{:S(2)}) collective-permute-start(bf16[64,1152]{1,0:T(8,128)(2,1)S(1)} %get-tuple-element.38), channel_id=1, source_target_pairs={{0,2},{1,3},{2,0},{3,1},{4,6},{5,7},{6,4},{7,5},{8,10},{9,11},{10,... | collective-permute-start | bytes 442376 | tf_op jit(solution)/shard_map/ppermute | solution.py:436
  56.4 20.8 %collective-permute-start.14 = (bf16[64,1152]{1,0:T(8,128)(2,1)S(1)}, bf16[64,1152]{1,0:T(8,128)(2,1)S(1)}, u32[]{:S(2)}, u32[]{:S(2)}) collective-permute-start(bf16[64,1152]{1,0:T(8,128)(2,1)S(1)} %get-tuple-element.39), channel_id=1, source_target_pairs={{0,3},{1,0},{2,1},{3,2},{4,7},{5,4},{6,5},{7,6},{8,11},{9,8},{10,9... | collective-permute-start | bytes 442376 | tf_op jit(solution)/shard_map/ppermute | solution.py:436
  59.3 17.9 %collective-permute-start.19 = (bf16[64,1024]{1,0:T(8,128)(2,1)S(1)}, bf16[64,1024]{1,0:T(8,128)(2,1)S(1)}, u32[]{:S(2)}, u32[]{:S(2)}) collective-permute-start(bf16[64,1024]{1,0:T(8,128)(2,1)S(1)} %get-tuple-element.47), channel_id=1, source_target_pairs={{0,2},{1,3},{2,0},{3,1},{4,6},{5,7},{6,4},{7,5},{8,10},{9,11},{10,... | collective-permute-start | bytes 393224 | tf_op jit(solution)/shard_map/ppermute | solution.py:436
  60.6 16.6 %collective-permute-start.20 = (bf16[64,1024]{1,0:T(8,128)(2,1)S(1)}, bf16[64,1024]{1,0:T(8,128)(2,1)S(1)}, u32[]{:S(2)}, u32[]{:S(2)}) collective-permute-start(bf16[64,1024]{1,0:T(8,128)(2,1)S(1)} %get-tuple-element.48), channel_id=1, source_target_pairs={{0,3},{1,0},{2,1},{3,2},{4,7},{5,4},{6,5},{7,6},{8,11},{9,8},{10,9... | collective-permute-start | bytes 393224 | tf_op jit(solution)/shard_map/ppermute | solution.py:436
  78.6 7.8 %collective-permute-start.23 = (bf16[64,1024]{1,0:T(8,128)(2,1)S(1)}, bf16[64,1024]{1,0:T(8,128)(2,1)S(1)}, u32[]{:S(2)}, u32[]{:S(2)}) collective-permute-start(bf16[64,1024]{1,0:T(8,128)(2,1)S(1)} %get-tuple-element.52), channel_id=1, source_target_pairs={{0,4},{4,0},{8,12},{12,8},{1,5},{5,1},{9,13},{13,9},{2,6},{6,2},{1... | collective-permute-start | bytes 393224 | tf_op jit(solution)/shard_map/ppermute | solution.py:443
  79.9 6.5 %collective-permute-start.21 = (bf16[64,1024]{1,0:T(8,128)(2,1)S(1)}, bf16[64,1024]{1,0:T(8,128)(2,1)S(1)}, u32[]{:S(2)}, u32[]{:S(2)}) collective-permute-start(bf16[64,1024]{1,0:T(8,128)(2,1)S(1)} %get-tuple-element.49), channel_id=1, source_target_pairs={{0,8},{4,12},{8,0},{12,4},{1,9},{5,13},{9,1},{13,5},{2,10},{6,14},... | collective-permute-start | bytes 393224 | tf_op jit(solution)/shard_map/ppermute | solution.py:443
  81.5 6.7 %collective-permute-start.22 = (bf16[64,1024]{1,0:T(8,128)(2,1)S(1)}, bf16[64,1024]{1,0:T(8,128)(2,1)S(1)}, u32[]{:S(2)}, u32[]{:S(2)}) collective-permute-start(bf16[64,1024]{1,0:T(8,128)(2,1)S(1)} %get-tuple-element.50), channel_id=1, source_target_pairs={{0,12},{4,8},{8,4},{12,0},{1,13},{5,9},{9,5},{13,1},{2,14},{6,10},... | collective-permute-start | bytes 393224 | tf_op jit(solution)/shard_map/ppermute | solution.py:443
  83.1 5.1 %collective-permute-start.17 = (bf16[64,1024]{1,0:T(8,128)(2,1)S(1)}, bf16[64,1024]{1,0:T(8,128)(2,1)S(1)}, u32[]{:S(2)}, u32[]{:S(2)}) collective-permute-start(bf16[64,1024]{1,0:T(8,128)(2,1)S(1)} %get-tuple-element.44), channel_id=1, source_target_pairs={{0,4},{4,0},{8,12},{12,8},{1,5},{5,1},{9,13},{13,9},{2,6},{6,2},{1... | collective-permute-start | bytes 393224 | tf_op jit(solution)/shard_map/ppermute | solution.py:443
  84.8 7.2 %collective-permute-start.15 = (bf16[64,1024]{1,0:T(8,128)(2,1)S(1)}, bf16[64,1024]{1,0:T(8,128)(2,1)S(1)}, u32[]{:S(2)}, u32[]{:S(2)}) collective-permute-start(bf16[64,1024]{1,0:T(8,128)(2,1)S(1)} %get-tuple-element.41), channel_id=1, source_target_pairs={{0,8},{4,12},{8,0},{12,4},{1,9},{5,13},{9,1},{13,5},{2,10},{6,14},... | collective-permute-start | bytes 393224 | tf_op jit(solution)/shard_map/ppermute | solution.py:443
  86.4 7.5 %collective-permute-start.16 = (bf16[64,1024]{1,0:T(8,128)(2,1)S(1)}, bf16[64,1024]{1,0:T(8,128)(2,1)S(1)}, u32[]{:S(2)}, u32[]{:S(2)}) collective-permute-start(bf16[64,1024]{1,0:T(8,128)(2,1)S(1)} %get-tuple-element.42), channel_id=1, source_target_pairs={{0,12},{4,8},{8,4},{12,0},{1,13},{5,9},{9,5},{13,1},{2,14},{6,10},... | collective-permute-start | bytes 393224 | tf_op jit(solution)/shard_map/ppermute | solution.py:443
  (1 other events, 0.7 us)
